TPU v7x, 512 devices: a whole 4x4x16 slice. The times are simulated.
512 devices in a mesh: space: 64 (over z, x), level: 8 (over y, core).
Axes of the slice: x: 4, y: 4, z: 16, core: 2. Of those that a mesh axis runs over, the one named last changes fastest.
Arguments:
- velocity: float32 [2, 64, 65536], P(None, 'level', 'space'), may hold values from -3 to 3
- density: float32 [64, 65536], P('level', 'space'), may hold values from -6 to 6
- elevation: float32 [65536], P('space'), may hold values from -3 to 3
- grad_weights: float32 [2, 6, 65536], P(None, None, 'space'), may hold values from -2.4 to 2.4
- lap_weights: float32 [6, 65536], P(None, 'space'), may hold values from 0.02 to 0.2
- coriolis: float32 [65536], P('space'), may hold values from 0.5 to 2
- node_area: float32 [65536], P('space'), may hold values from 1 to 100, as said below
- thickness: float32 [64], P('level'), may hold values from 0.5 to 2
- send_list: int32 [64, 256], P('space'), may hold values from 0 to 1023
- neighbours: int32 [6, 65536], P(None, 'space'), may hold values from 0 to 1279
- bottom: int32 [65536], P('space'), may hold values from 0 to 64, as said below
Outputs:
- velocity_out: float32 [2, 64, 65536], P(None, 'level', 'space')
- density_out: float32 [64, 65536], P('level', 'space')
- elevation_out: float32 [65536], P('space')
- volume_drift: float32 [4], replicated
Inputs may be any that keep to these rules, and one draw needn't show every extreme that they name: `send_list`: local node numbers within the sending partition; the first 128 go to the partition one below along space, the other 128 to the one above. `neighbours`: slots below 1024 are the partition's own nodes; the next 128 are halo slots filled from the partition below, the last 128 from the partition above. Levels of a node are wet from the surface down to bottom - 1; a node with 0 is dry. Some partitions are shallower than others. `node_area`: positive areas.
All inputs are finite; a program needn't handle non-finite values.
Results may differ from a plain program's by a relative error of at most 0.00013.
Values sent between devices are 32-bit elements; how exact they have to be, the bound alone decides.
A program may use at most 64 MiB of HBM per device.

v0:
```python
import jax
import jax.numpy as jnp
from jax import lax
from jax.sharding import PartitionSpec as P

STEPS = 4


time_step = 0.1
buoyancy = 0.5
drag_rate = 0.5


def extended_2(array, sides, width):
    for axis, dim in sides:
        devices, length = (lax.axis_size(axis), array.shape[dim])
        up = [(i, (i + 1) % devices) for i in range(devices - 1)]
        down = [(j, i) for i, j in up]
        last = lax.slice_in_dim(array, length - width, length, axis=dim)
        first = lax.slice_in_dim(array, 0, width, axis=dim)
        before = lax.ppermute(last, axis, up)
        after = lax.ppermute(first, axis, down)
        array = jnp.concatenate([before, array, after], axis=dim)
    return array


def in_order(pieces, dim):
    lengths = list(pieces.shape[1:])
    lengths[dim] *= pieces.shape[0]
    return jnp.moveaxis(pieces, 0, dim).reshape(lengths)


def sent_to_all(array, axis):
    devices = lax.axis_size(axis)
    return lax.all_to_all(
        jnp.broadcast_to(array[None], (devices, *array.shape)), axis, 0, 0, tiled=True
    )


def gathered_copies(array, axis, dim):
    return in_order(sent_to_all(array, axis), dim)


def of_everyone(array, axis):
    return sent_to_all(array, axis).sum(axis=0)


def in_one(arrays, axis):
    ends = [0]
    for a in arrays:
        ends.append(ends[-1] + a.size)
    total = of_everyone(jnp.concatenate([a.ravel() for a in arrays]), axis)
    return tuple((total[b:e].reshape(a.shape) for a, b, e in zip(arrays, ends, ends[1:])))


def neighbour_terms(fields, neighbours, weights):
    node_count = neighbours.shape[1]
    near_count = neighbours.shape[0]
    node_major = fields.T
    nearby = jnp.take(node_major, neighbours.reshape(-1), axis=0)
    nearby = nearby.reshape(near_count, node_count, fields.shape[0])
    differ = nearby - node_major[None, :node_count]
    return tuple(
        (
            jnp.einsum("knr,kn->rn", differ, weight, precision=lax.Precision.HIGHEST)
            for weight in weights
        )
    )


def local(
    velocity,
    density,
    elevation,
    grad_weights,
    lap_weights,
    coriolis,
    node_area,
    thickness,
    send_list,
    neighbours,
    bottom,
):
    level_count = density.shape[0]
    node_count = density.shape[1]
    half_slots = send_list.shape[1] // 2
    level_first = lax.axis_index("level") * level_count
    level_ids = level_first + jnp.arange(level_count, dtype=jnp.int32)
    wet_cells = (level_ids[:, None] < bottom[None, :]).astype(jnp.float32)
    at_floor = (level_ids[:, None] == bottom[None, :] - 1).astype(jnp.float32)
    wet_nodes = (bottom > 0).astype(jnp.float32)
    space_rank = lax.axis_index("space")
    space_count = lax.axis_size("space")
    slot_ids = jnp.arange(2 * half_slots, dtype=jnp.int32)
    halo_valid = jnp.where(
        slot_ids < half_slots, space_rank > 0, space_rank < space_count - 1
    ).astype(jnp.float32)
    valid_wide = jnp.concatenate([jnp.ones((node_count,), jnp.float32), halo_valid])
    valid_near = jnp.take(valid_wide, neighbours)
    weights = (grad_weights[0] * valid_near, grad_weights[1] * valid_near, lap_weights * valid_near)
    outgoing_ids = send_list[0]
    area_local = jnp.sum(node_area * wet_nodes)
    velocity = velocity * wet_cells[None]
    volume_terms = []
    for counter in range(STEPS):
        stacked = jnp.concatenate(
            [velocity.reshape(2 * level_count, node_count), density, elevation[None]], axis=0
        )
        outgoing = jnp.take(stacked.T, outgoing_ids, axis=0).T
        padded = extended_2(outgoing, (("space", 1),), half_slots)
        remote = jnp.concatenate([padded[:, :half_slots], padded[:, 3 * half_slots :]], axis=1)
        extended = jnp.concatenate([stacked, remote], axis=1)
        wide_velocity = extended[: 2 * level_count].reshape(2, level_count, extended.shape[1])
        wide_density = extended[2 * level_count : 3 * level_count]
        weighted = wide_density * thickness[:, None]
        own_total = jnp.sum(weighted, axis=0)
        transport_part = jnp.einsum(
            "cle,l->ce", wide_velocity, thickness, precision=lax.Precision.HIGHEST
        )
        column_part = jnp.concatenate([own_total[None], transport_part], axis=0)[None]
        gathered = gathered_copies(column_part, "level", 0)
        below_mask = (
            jnp.arange(gathered.shape[0], dtype=jnp.int32) < lax.axis_index("level")
        ).astype(jnp.float32)
        above_sum = jnp.einsum(
            "g,ge->e", below_mask, gathered[:, 0], precision=lax.Precision.HIGHEST
        )
        transport = jnp.sum(gathered[:, 1:], axis=0)
        pressure = buoyancy * (above_sum[None] + jnp.cumsum(weighted, axis=0) - 0.5 * weighted)
        fields = jnp.concatenate([extended, pressure, transport], axis=0)
        gradient_east, gradient_north, laplace = neighbour_terms(fields, neighbours, weights)
        elev_row = 3 * level_count
        press_first = 3 * level_count + 1
        flow_row = 4 * level_count + 1
        diverge = gradient_east[flow_row] + gradient_north[flow_row + 1]
        volume_term = jnp.sum(node_area * wet_nodes * diverge)
        new_elevation = elevation - time_step * wet_nodes * diverge
        volume_terms.append(volume_term)
        east_speed = velocity[0]
        north_speed = velocity[1]
        push_east = (
            -gradient_east[elev_row][None]
            - gradient_east[press_first : press_first + level_count]
            + coriolis[None] * north_speed
            + laplace[:level_count]
            - drag_rate * at_floor * east_speed
        )
        push_north = (
            -gradient_north[elev_row][None]
            - gradient_north[press_first : press_first + level_count]
            - coriolis[None] * east_speed
            + laplace[level_count : 2 * level_count]
            - drag_rate * at_floor * north_speed
        )
        density = density + time_step * (
            laplace[2 * level_count : 3 * level_count]
            - east_speed * gradient_east[2 * level_count : 3 * level_count]
            - north_speed * gradient_north[2 * level_count : 3 * level_count]
        )
        velocity = wet_cells[None] * (velocity + time_step * jnp.stack([push_east, push_north]))
        elevation = new_elevation
    summed, area_total = in_one((jnp.stack(volume_terms), area_local), "space")
    drifts = summed / area_total
    elevation = elevation + time_step * jnp.sum(drifts)
    return (velocity, density, elevation, drifts)


def solution(mesh):
    return jax.shard_map(
        local,
        mesh=mesh,
        in_specs=(
            P(None, "level", "space"),
            P("level", "space"),
            P("space"),
            P(None, None, "space"),
            P(None, "space"),
            P("space"),
            P("space"),
            P("level"),
            P("space", None),
            P(None, "space"),
            P("space"),
        ),
        out_specs=(P(None, "level", "space"), P("level", "space"), P("space"), P()),
        check_vma=False,
    )
```

profile of v0, /device:TPU:1, one launch (start us, length us, event | category | flops | bytes accessed | tf_op | source)
XLA Modules:
  0.0 293.5 jit_solution(2174263429301038482)
XLA Ops:
  5.5 3.9 %collective-permute-start = (f32[25,128]{0,1:T(8,128)S(1)}, f32[25,128]{0,1:T(8,128)S(1)}, u32[]{:S(2)}, u32[]{:S(2)}) collective-permute-start(f32[25,128]{0,1:T(8,128)S(1)} %get-tuple-element.73), channel_id=1, source_target_pairs={{0,8},{8,16},{16,24},{24,32},{32,40},{40,48},{48,56},{56,64},{64,7... | collective-permute-start | bytes 38408 | tf_op jit(solution)/shard_map/ppermute | solution.py:21
  13.3 34.3 %gather_fusion = f32[6144]{0:T(1024)S(1)} fusion(f32[1280]{0:T(1024)S(1)} %pad_convert_fusion, s32[6144]{0:T(1024)S(1)} %broadcast_clamp_fusion), kind=kCustom, calls=%fused_computation.8 | custom fusion | bytes 73728 | tf_op jit(solution)/shard_map/jit(_take)/gather | solution.py:99
  49.0 7.5 %all-to-all-start = ((f32[8,1,3,1280]{3,1,2,0:T(1,128)}), f32[8,1,3,1280]{3,1,2,0:T(1,128)S(1)}, u32[]{:S(2)}, u32[]{:S(2)}) async-start(f32[8,1,3,1280]{3,1,2,0:T(1,128)} %broadcast_in_dim.66), calls=%async_computation | async-start | bytes 245760 | tf_op jit(solution)/shard_map/all_to_all | solution.py:35
  56.5 5.1 %all-to-all-done = f32[8,1,3,1280]{3,1,2,0:T(1,128)S(1)} async-done(((f32[8,1,3,1280]{3,1,2,0:T(1,128)}), f32[8,1,3,1280]{3,1,2,0:T(1,128)S(1)}, u32[]{:S(2)}, u32[]{:S(2)}) %all-to-all-start) | async-done | bytes 122912 | tf_op jit(solution)/shard_map/all_to_all | solution.py:35
  62.2 20.9 %gather_fusion.2 = f32[6144,35]{1,0:T(8,128)} fusion(f32[1280,35]{1,0:T(8,128)S(1)} %bitcast.269, s32[6144]{0:T(1024)S(1)} %fusion.68), kind=kCustom, calls=%fused_computation.1.clone | custom fusion | bytes 1744896 | tf_op jit(solution)/shard_map/jit(_take)/gather | solution.py:60
  83.1 4.7 %broadcast_select_fusion.3 = f32[6144,35]{1,0:T(8,128)S(1)} fusion(f32[6144,35]{1,0:T(8,128)} %gather_fusion.2, pred[6144]{0:T(1024)(128)(4,1)S(1)} %compare_and_fusion), kind=kLoop, calls=%fused_computation.24 | loop fusion | flops 215040 | bytes 1726464 | tf_op jit(solution)/shard_map/jit(_take)/select_n | solution.py:60
  92.8 4.3 %collective-permute-start.2 = (f32[25,128]{0,1:T(8,128)S(1)}, f32[25,128]{0,1:T(8,128)S(1)}, u32[]{:S(2)}, u32[]{:S(2)}) collective-permute-start(f32[25,128]{0,1:T(8,128)S(1)} %get-tuple-element.71), channel_id=1, source_target_pairs={{0,8},{8,16},{16,24},{24,32},{32,40},{40,48},{48,56},{56,64},{64,7... | collective-permute-start | bytes 38408 | tf_op jit(solution)/shard_map/ppermute | solution.py:21
  103.2 5.6 %all-to-all-start.1 = ((f32[8,1,3,1280]{3,1,2,0:T(1,128)}), f32[8,1,3,1280]{3,1,2,0:T(1,128)S(1)}, u32[]{:S(2)}, u32[]{:S(2)}) async-start(f32[8,1,3,1280]{3,1,2,0:T(1,128)} %broadcast_in_dim.69), calls=%async_computation.1 | async-start | bytes 245760 | tf_op jit(solution)/shard_map/all_to_all | solution.py:35
  108.9 5.1 %all-to-all-done.1 = f32[8,1,3,1280]{3,1,2,0:T(1,128)S(1)} async-done(((f32[8,1,3,1280]{3,1,2,0:T(1,128)}), f32[8,1,3,1280]{3,1,2,0:T(1,128)S(1)}, u32[]{:S(2)}, u32[]{:S(2)}) %all-to-all-start.1) | async-done | bytes 122912 | tf_op jit(solution)/shard_map/all_to_all | solution.py:35
  114.5 20.9 %gather_fusion.4 = f32[6144,35]{1,0:T(8,128)} fusion(f32[1280,35]{1,0:T(8,128)S(1)} %bitcast.270, s32[6144]{0:T(1024)S(1)} %fusion.68), kind=kCustom, calls=%fused_computation.5.clone | custom fusion | bytes 1744896 | tf_op jit(solution)/shard_map/jit(_take)/gather | solution.py:60
  135.4 4.7 %broadcast_select_fusion.2 = f32[6144,35]{1,0:T(8,128)S(1)} fusion(f32[6144,35]{1,0:T(8,128)} %gather_fusion.4, pred[6144]{0:T(1024)(128)(4,1)S(1)} %compare_and_fusion), kind=kLoop, calls=%fused_computation.23 | loop fusion | flops 215040 | bytes 1726464 | tf_op jit(solution)/shard_map/jit(_take)/select_n | solution.py:60
  148.2 4.4 %collective-permute-done.5 = f32[25,128]{0,1:T(8,128)S(1)} collective-permute-done((f32[25,128]{0,1:T(8,128)S(1)}, f32[25,128]{0,1:T(8,128)S(1)}, u32[]{:S(2)}, u32[]{:S(2)}) %collective-permute-start.5) | collective-permute-done | bytes 12832 | tf_op jit(solution)/shard_map/ppermute | solution.py:22
  153.7 5.3 %all-to-all-start.2 = ((f32[8,1,3,1280]{3,1,2,0:T(1,128)}), f32[8,1,3,1280]{3,1,2,0:T(1,128)S(1)}, u32[]{:S(2)}, u32[]{:S(2)}) async-start(f32[8,1,3,1280]{3,1,2,0:T(1,128)} %broadcast_in_dim.72), calls=%async_computation.2 | async-start | bytes 245760 | tf_op jit(solution)/shard_map/all_to_all | solution.py:35
  159.1 5.1 %all-to-all-done.2 = f32[8,1,3,1280]{3,1,2,0:T(1,128)S(1)} async-done(((f32[8,1,3,1280]{3,1,2,0:T(1,128)}), f32[8,1,3,1280]{3,1,2,0:T(1,128)S(1)}, u32[]{:S(2)}, u32[]{:S(2)}) %all-to-all-start.2) | async-done | bytes 122912 | tf_op jit(solution)/shard_map/all_to_all | solution.py:35
  164.7 20.9 %gather_fusion.6 = f32[6144,35]{1,0:T(8,128)} fusion(f32[1280,35]{1,0:T(8,128)S(1)} %bitcast.272, s32[6144]{0:T(1024)S(1)} %fusion.68), kind=kCustom, calls=%fused_computation.6.clone | custom fusion | bytes 1744896 | tf_op jit(solution)/shard_map/jit(_take)/gather | solution.py:60
  185.7 4.7 %broadcast_select_fusion.1 = f32[6144,35]{1,0:T(8,128)S(1)} fusion(f32[6144,35]{1,0:T(8,128)} %gather_fusion.6, pred[6144]{0:T(1024)(128)(4,1)S(1)} %compare_and_fusion), kind=kLoop, calls=%fused_computation.22 | loop fusion | flops 215040 | bytes 1726464 | tf_op jit(solution)/shard_map/jit(_take)/select_n | solution.py:60
  195.4 5.8 %collective-permute-start.6 = (f32[25,128]{0,1:T(8,128)S(1)}, f32[25,128]{0,1:T(8,128)S(1)}, u32[]{:S(2)}, u32[]{:S(2)}) collective-permute-start(f32[25,128]{0,1:T(8,128)S(1)} %get-tuple-element.67), channel_id=1, source_target_pairs={{0,8},{8,16},{16,24},{24,32},{32,40},{40,48},{48,56},{56,64},{64,7... | collective-permute-start | bytes 38408 | tf_op jit(solution)/shard_map/ppermute | solution.py:21
  202.5 3.9 %collective-permute-done.7 = f32[25,128]{0,1:T(8,128)S(1)} collective-permute-done((f32[25,128]{0,1:T(8,128)S(1)}, f32[25,128]{0,1:T(8,128)S(1)}, u32[]{:S(2)}, u32[]{:S(2)}) %collective-permute-start.7) | collective-permute-done | bytes 12832 | tf_op jit(solution)/shard_map/ppermute | solution.py:22
  207.6 5.3 %all-to-all-start.3 = ((f32[8,1,3,1280]{3,1,2,0:T(1,128)}), f32[8,1,3,1280]{3,1,2,0:T(1,128)S(1)}, u32[]{:S(2)}, u32[]{:S(2)}) async-start(f32[8,1,3,1280]{3,1,2,0:T(1,128)} %broadcast_in_dim.129), calls=%async_computation.3 | async-start | bytes 245760 | tf_op jit(solution)/shard_map/all_to_all | solution.py:35
  212.9 5.1 %all-to-all-done.3 = f32[8,1,3,1280]{3,1,2,0:T(1,128)S(1)} async-done(((f32[8,1,3,1280]{3,1,2,0:T(1,128)}), f32[8,1,3,1280]{3,1,2,0:T(1,128)S(1)}, u32[]{:S(2)}, u32[]{:S(2)}) %all-to-all-start.3) | async-done | bytes 122912 | tf_op jit(solution)/shard_map/all_to_all | solution.py:35
  218.6 20.9 %gather_fusion.8 = f32[6144,35]{1,0:T(8,128)} fusion(f32[1280,35]{1,0:T(8,128)S(1)} %bitcast.266, s32[6144]{0:T(1024)S(1)} %fusion.68), kind=kCustom, calls=%fused_computation.7.clone | custom fusion | bytes 1744896 | tf_op jit(solution)/shard_map/jit(_take)/gather | solution.py:60
  239.5 4.7 %broadcast_select_fusion = f32[6144,35]{1,0:T(8,128)S(1)} fusion(f32[6144,35]{1,0:T(8,128)} %gather_fusion.8, pred[6144]{0:T(1024)(128)(4,1)S(1)} %compare_and_fusion), kind=kLoop, calls=%fused_computation.21 | loop fusion | flops 215040 | bytes 1726464 | tf_op jit(solution)/shard_map/jit(_take)/select_n | solution.py:60
  252.5 23.6 %all-to-all-start.4 = ((f32[64,1,5]{2,1,0:T(1,128)}), f32[64,1,5]{2,1,0:T(1,128)S(1)}, u32[]{:S(2)}, u32[]{:S(2)}) async-start(f32[64,1,5]{2,1,0:T(1,128)} %broadcast_in_dim.130), calls=%async_computation.4 | async-start | bytes 65536 | tf_op jit(solution)/shard_map/all_to_all | solution.py:35
  277.6 12.1 %all-to-all-done.4 = f32[64,1,5]{2,1,0:T(1,128)S(1)} async-done(((f32[64,1,5]{2,1,0:T(1,128)}), f32[64,1,5]{2,1,0:T(1,128)S(1)}, u32[]{:S(2)}, u32[]{:S(2)}) %all-to-all-start.4) | async-done | bytes 1312 | tf_op jit(solution)/shard_map/all_to_all | solution.py:35
  (175 shorter events, 52.7 us)
Async XLA Ops:
  5.5 42.2 %collective-permute-start = (f32[25,128]{0,1:T(8,128)S(1)}, f32[25,128]{0,1:T(8,128)S(1)}, u32[]{:S(2)}, u32[]{:S(2)}) collective-permute-start(f32[25,128]{0,1:T(8,128)S(1)} %get-tuple-element.73), channel_id=1, source_target_pairs={{0,8},{8,16},{16,24},{24,32},{32,40},{40,48},{48,56},{56,64},{64,7... | collective-permute-start | bytes 38408 | tf_op jit(solution)/shard_map/ppermute | solution.py:21
  9.4 38.4 %collective-permute-start.1 = (f32[25,128]{0,1:T(8,128)S(1)}, f32[25,128]{0,1:T(8,128)S(1)}, u32[]{:S(2)}, u32[]{:S(2)}) collective-permute-start(f32[25,128]{0,1:T(8,128)S(1)} %get-tuple-element.74), channel_id=1, source_target_pairs={{8,0},{16,8},{24,16},{32,24},{40,32},{48,40},{56,48},{64,56},{72,6... | collective-permute-start | bytes 38408 | tf_op jit(solution)/shard_map/ppermute | solution.py:22
  13.2 34.4 %copy-start.5 = (f32[2,6,1024]{2,0,1:T(2,128)S(1)}, f32[2,6,1024]{2,0,1:T(2,128)}, u32[]{:S(2)}) copy-start(f32[2,6,1024]{2,0,1:T(2,128)} %param.18) | copy-start | bytes 147460
  13.2 34.4 %copy-start.2 = (s32[6,1024]{1,0:T(8,128)S(1)}, s32[6,1024]{1,0:T(8,128)}, u32[]{:S(2)}) copy-start(s32[6,1024]{1,0:T(8,128)} %param.24) | copy-start | bytes 73732
  13.2 34.4 %copy-start.7 = (f32[6,1024]{1,0:T(8,128)S(1)}, f32[6,1024]{1,0:T(8,128)}, u32[]{:S(2)}) copy-start(f32[6,1024]{1,0:T(8,128)} %param.19) | copy-start | bytes 73732
  13.2 34.7 %copy-start.1 = (f32[8,1024]{1,0:T(8,128)S(1)}, f32[8,1024]{1,0:T(8,128)}, u32[]{:S(2)}) copy-start(f32[8,1024]{1,0:T(8,128)} %param.16) | copy-start | bytes 98308
  13.2 34.7 %copy-start.4 = (f32[1024]{0:T(1024)S(1)}, f32[1024]{0:T(1024)}, u32[]{:S(2)}) copy-start(f32[1024]{0:T(1024)} %param.17) | copy-start | bytes 12292
  13.2 34.6 %copy-start.8 = (f32[8]{0:T(128)S(1)}, f32[8]{0:T(128)}, u32[]{:S(2)}) copy-start(f32[8]{0:T(128)} %param.22) | copy-start | bytes 100
  13.3 43.2 %copy-start.6 = (s32[1024]{0:T(1024)S(1)}, s32[1024]{0:T(1024)}, u32[]{:S(2)}) copy-start(s32[1024]{0:T(1024)} %param.25) | copy-start | bytes 12292
  49.0 12.7 %all-to-all-start = ((f32[8,1,3,1280]{3,1,2,0:T(1,128)}), f32[8,1,3,1280]{3,1,2,0:T(1,128)S(1)}, u32[]{:S(2)}, u32[]{:S(2)}) async-start(f32[8,1,3,1280]{3,1,2,0:T(1,128)} %broadcast_in_dim.66), calls=%async_computation | async-start | bytes 245760 | tf_op jit(solution)/shard_map/all_to_all | solution.py:35
  87.7 3.8 %copy-start.3 = (f32[1024]{0:T(1024)S(1)}, f32[1024]{0:T(1024)}, u32[]{:S(2)}) copy-start(f32[1024]{0:T(1024)} %param.20) | copy-start | bytes 12292
  87.8 3.9 %copy-start = (f32[2,8,1024]{2,1,0:T(8,128)S(1)}, f32[2,8,1024]{2,1,0:T(8,128)}, u32[]{:S(2)}) copy-start(f32[2,8,1024]{2,1,0:T(8,128)} %param.15) | copy-start | bytes 196612
  92.8 5.6 %collective-permute-start.2 = (f32[25,128]{0,1:T(8,128)S(1)}, f32[25,128]{0,1:T(8,128)S(1)}, u32[]{:S(2)}, u32[]{:S(2)}) collective-permute-start(f32[25,128]{0,1:T(8,128)S(1)} %get-tuple-element.71), channel_id=1, source_target_pairs={{0,8},{8,16},{16,24},{24,32},{32,40},{40,48},{48,56},{56,64},{64,7... | collective-permute-start | bytes 38408 | tf_op jit(solution)/shard_map/ppermute | solution.py:21
  97.1 5.0 %collective-permute-start.3 = (f32[25,128]{0,1:T(8,128)S(1)}, f32[25,128]{0,1:T(8,128)S(1)}, u32[]{:S(2)}, u32[]{:S(2)}) collective-permute-start(f32[25,128]{0,1:T(8,128)S(1)} %get-tuple-element.72), channel_id=1, source_target_pairs={{8,0},{16,8},{24,16},{32,24},{40,32},{48,40},{56,48},{64,56},{72,6... | collective-permute-start | bytes 38408 | tf_op jit(solution)/shard_map/ppermute | solution.py:22
  103.2 10.7 %all-to-all-start.1 = ((f32[8,1,3,1280]{3,1,2,0:T(1,128)}), f32[8,1,3,1280]{3,1,2,0:T(1,128)S(1)}, u32[]{:S(2)}, u32[]{:S(2)}) async-start(f32[8,1,3,1280]{3,1,2,0:T(1,128)} %broadcast_in_dim.69), calls=%async_computation.1 | async-start | bytes 245760 | tf_op jit(solution)/shard_map/all_to_all | solution.py:35
  145.2 3.0 %collective-permute-start.4 = (f32[25,128]{0,1:T(8,128)S(1)}, f32[25,128]{0,1:T(8,128)S(1)}, u32[]{:S(2)}, u32[]{:S(2)}) collective-permute-start(f32[25,128]{0,1:T(8,128)S(1)} %get-tuple-element.69), channel_id=1, source_target_pairs={{0,8},{8,16},{16,24},{24,32},{32,40},{40,48},{48,56},{56,64},{64,7... | collective-permute-start | bytes 38408 | tf_op jit(solution)/shard_map/ppermute | solution.py:21
  146.8 5.8 %collective-permute-start.5 = (f32[25,128]{0,1:T(8,128)S(1)}, f32[25,128]{0,1:T(8,128)S(1)}, u32[]{:S(2)}, u32[]{:S(2)}) collective-permute-start(f32[25,128]{0,1:T(8,128)S(1)} %get-tuple-element.70), channel_id=1, source_target_pairs={{8,0},{16,8},{24,16},{32,24},{40,32},{48,40},{56,48},{64,56},{72,6... | collective-permute-start | bytes 38408 | tf_op jit(solution)/shard_map/ppermute | solution.py:22
  153.7 10.5 %all-to-all-start.2 = ((f32[8,1,3,1280]{3,1,2,0:T(1,128)}), f32[8,1,3,1280]{3,1,2,0:T(1,128)S(1)}, u32[]{:S(2)}, u32[]{:S(2)}) async-start(f32[8,1,3,1280]{3,1,2,0:T(1,128)} %broadcast_in_dim.72), calls=%async_computation.2 | async-start | bytes 245760 | tf_op jit(solution)/shard_map/all_to_all | solution.py:35
  195.4 7.1 %collective-permute-start.6 = (f32[25,128]{0,1:T(8,128)S(1)}, f32[25,128]{0,1:T(8,128)S(1)}, u32[]{:S(2)}, u32[]{:S(2)}) collective-permute-start(f32[25,128]{0,1:T(8,128)S(1)} %get-tuple-element.67), channel_id=1, source_target_pairs={{0,8},{8,16},{16,24},{24,32},{32,40},{40,48},{48,56},{56,64},{64,7... | collective-permute-start | bytes 38408 | tf_op jit(solution)/shard_map/ppermute | solution.py:21
  201.2 5.3 %collective-permute-start.7 = (f32[25,128]{0,1:T(8,128)S(1)}, f32[25,128]{0,1:T(8,128)S(1)}, u32[]{:S(2)}, u32[]{:S(2)}) collective-permute-start(f32[25,128]{0,1:T(8,128)S(1)} %get-tuple-element.68), channel_id=1, source_target_pairs={{8,0},{16,8},{24,16},{32,24},{40,32},{48,40},{56,48},{64,56},{72,6... | collective-permute-start | bytes 38408 | tf_op jit(solution)/shard_map/ppermute | solution.py:22
  207.6 10.5 %all-to-all-start.3 = ((f32[8,1,3,1280]{3,1,2,0:T(1,128)}), f32[8,1,3,1280]{3,1,2,0:T(1,128)S(1)}, u32[]{:S(2)}, u32[]{:S(2)}) async-start(f32[8,1,3,1280]{3,1,2,0:T(1,128)} %broadcast_in_dim.129), calls=%async_computation.3 | async-start | bytes 245760 | tf_op jit(solution)/shard_map/all_to_all | solution.py:35
  244.2 3.6 %copy-start.9 = (f32[1024]{0:T(1024)S(1)}, f32[1024]{0:T(1024)}, u32[]{:S(2)}) copy-start(f32[1024]{0:T(1024)} %param.21) | copy-start | bytes 12292
  252.5 37.2 %all-to-all-start.4 = ((f32[64,1,5]{2,1,0:T(1,128)}), f32[64,1,5]{2,1,0:T(1,128)S(1)}, u32[]{:S(2)}, u32[]{:S(2)}) async-start(f32[64,1,5]{2,1,0:T(1,128)} %broadcast_in_dim.130), calls=%async_computation.4 | async-start | bytes 65536 | tf_op jit(solution)/shard_map/all_to_all | solution.py:35
where the time goes:
time: 295 us; the launch traced here: 294 us
  local copies, waits for them, and re-layouts  134 us (45%)
  starting transfers between devices  67.9 us (23%)
  waiting for transfers between devices  44.6 us (15%)
  other arithmetic  43.2 us (15%)
    gather x4, local copies, waits for them, and re-layouts, neighbour_terms(): nearby = jnp.take(node_major, neighbours.reshape(-1), axis=0)  83.6 us
    all_to_all x5, starting transfers between devices, sent_to_all(): lax.all_to_all(jnp.broadcast_to(array[None], (devices, *array.shape)), ax...  47.1 us
    gather x2, local copies, waits for them, and re-layouts, local(): valid_near = jnp.take(valid_wide, neighbours)  34.3 us
    all_to_all x5, waiting for transfers between devices, sent_to_all(): lax.all_to_all(jnp.broadcast_to(array[None], (devices, *array.shape)), ax...  32.6 us
    select_n x4, other arithmetic, neighbour_terms(): nearby = jnp.take(node_major, neighbours.reshape(-1), axis=0)  18.7 us
    ppermute x4, starting transfers between devices, extended_2(): before = lax.ppermute(last, axis, up)  15.6 us
    unnamed x5, other arithmetic  12.7 us
    ppermute x4, waiting for transfers between devices, extended_2(): after = lax.ppermute(first, axis, down)  12 us
  transfers between devices with their start and end apart: 13, of which 8 were waited for; matrix products, arithmetic and copies ran while one was open for 13% of the time, Pallas kernels for 0%

commit v1 on v0

v1 whole, which is shorter than its diff:
```python
import jax
import jax.numpy as jnp
from jax import lax
from jax.experimental import pallas as pl
from jax.experimental.pallas import tpu as pltpu
from jax.sharding import PartitionSpec as P

MESH = pl.DeviceIdType.MESH
STEPS = 4
K = 6
TILES = 8
LANES = 128
X_CHIPS = 4
DT = 0.1
BUOYANCY = 0.5
DRAG = 0.5

_LANE_GATHER = lax.GatherDimensionNumbers(
    offset_dims=(),
    collapsed_slice_dims=(1,),
    start_index_map=(1,),
    operand_batching_dims=(0,),
    start_indices_batching_dims=(0,),
)


def lane_gather(x, idx):
    return lax.gather(
        x, idx[..., None], _LANE_GATHER, (1, 1), mode=lax.GatherScatterMode.PROMISE_IN_BOUNDS
    )


def wide(row):
    return jnp.broadcast_to(row, (8, LANES))


def kernel(
    n_space,
    n_level,
    vel_ref,
    rho_ref,
    eta_ref,
    grad_ref,
    lap_ref,
    cor_ref,
    area_ref,
    thick_ref,
    send_ref,
    nb_ref,
    bot_ref,
    vel_out,
    rho_out,
    eta_out,
    drift_out,
    nbc,
    wts,
    x,
    ploc,
    part,
    near,
    q,
    dq,
    eta,
    etah,
    vv,
    lsend,
    lrecv,
    usend,
    urecv,
    rsend,
    rrecv,
    gsend,
    grecv,
    ssend,
    srecv,
    zsend,
    zrecv,
    xsend,
    xrecv,
    lsem,
    usem,
    rsem,
    gsem,
    ssem,
    zsem,
    tok,
):
    p = lax.axis_index("space")
    g = lax.axis_index("level")
    n_z = n_space // X_CHIPS
    up = lax.rem(p + 1, n_space)
    down = lax.rem(p + n_space - 1, n_space)
    level_peers = [lax.rem(g + d, n_level) for d in range(n_level)]

    def z_peer(d):
        return lax.rem(p + d * X_CHIPS, n_space)

    px = lax.rem(p, X_CHIPS)

    def x_peer(d):
        return p - px + lax.rem(px + d, X_CHIPS)

    barrier = pltpu.get_barrier_semaphore()
    count = 0

    def greet(a, b):
        pl.semaphore_signal(barrier, inc=1, device_id=(a, b), device_id_type=MESH)

    for d in range(n_level):
        greet(up, level_peers[d])
        greet(down, level_peers[d])
        count += 2
        if d:
            greet(p, level_peers[d])
            count += 1
    for d in (1, n_z - 1):
        greet(z_peer(d), g)
        count += 1
    for d in range(1, X_CHIPS):
        greet(x_peer(d), g)
        count += 1

    sub = lax.broadcasted_iota(jnp.int32, (8, LANES), 0)
    lane = lax.broadcasted_iota(jnp.int32, (8, LANES), 1)
    th = jnp.zeros((8, LANES), jnp.float32)
    for l in range(8):
        th = jnp.where(sub == l, thick_ref[l], th)
    level_id = sub + g * 8
    send_idx = [send_ref[:, side * LANES : (side + 1) * LANES] for side in range(2)]
    send_lane = [wide(i & (LANES - 1)) for i in send_idx]
    send_tile = [wide(i >> 7) for i in send_idx]

    def listed_levels(tiles, side):
        out = lane_gather(tiles[0], send_lane[side])
        for t in range(1, TILES):
            out = jnp.where(send_tile[side] == t, lane_gather(tiles[t], send_lane[side]), out)
        return out

    def listed_nodes(compact, side):
        got = lane_gather(compact, send_lane[side])
        return jnp.sum(jnp.where(send_tile[side] == sub, got, 0.0), axis=0, keepdims=True)

    def column(rho_tile):
        weighted = rho_tile * th
        total = weighted
        for shift in (1, 2, 4):
            total = total + jnp.where(sub >= shift, pltpu.roll(total, shift, 0), 0.0)
        return BUOYANCY * (total - 0.5 * weighted), total[7:8]

    def copy(src, dst, sems, i, a, b):
        return pltpu.make_async_remote_copy(
            src_ref=src,
            dst_ref=dst,
            send_sem=sems.at[0, i],
            recv_sem=sems.at[1, i],
            device_id=(a, b),
            device_id_type=MESH,
        )

    def arrived(buf, sems, i):
        pltpu.make_async_copy(buf, buf, sems.at[1, i]).wait()

    def left(buf, sems, i):
        pltpu.make_async_copy(buf, buf, sems.at[0, i]).wait()

    def send_velocity(s):
        for side in range(2):
            for c in range(2):
                usend[s, side, c] = listed_levels([x[c, d] for d in range(TILES)], side)
        copy(usend.at[s, 0], urecv.at[s, 1], usem, s, down, g).start()
        copy(usend.at[s, 1], urecv.at[s, 0], usem, s, up, g).start()

    def send_density(s):
        tiles = [x[2, d] for d in range(TILES)]
        for side in range(2):
            got = listed_levels(tiles, side)
            rsend[s, side] = got
            gsend[s, side, 0:1] = jnp.sum(got * th, axis=0, keepdims=True)
            gsend[s, side, 1:2] = listed_nodes(lsend[s, 1], side)
        copy(rsend.at[s, 0], rrecv.at[s, 1], rsem, s, down, g).start()
        copy(rsend.at[s, 1], rrecv.at[s, 0], rsem, s, up, g).start()
        for d in range(n_level):
            copy(gsend.at[s, 0], grecv.at[s, 1, d], gsem, s, down, level_peers[d]).start()
            copy(gsend.at[s, 1], grecv.at[s, 0, d], gsem, s, up, level_peers[d]).start()
        for d in range(TILES):
            ploc[d], lsend[s, 0, d : d + 1] = column(tiles[d])
        send_level(s)

    def send_level(s):
        for d in range(1, n_level):
            copy(lsend.at[s], lrecv.at[s, d - 1], lsem, s, p, level_peers[d]).start()

    for d in range(TILES):
        cols = slice(d * LANES, (d + 1) * LANES)
        wet = level_id < wide(bot_ref[d : d + 1])
        for c in range(2):
            x[c, d] = jnp.where(wet, vel_ref[c, :, cols], 0.0)
        x[2, d] = rho_ref[:, cols]
    eta[...] = eta_ref[...]
    wet_nodes = (bot_ref[...] > 0).astype(jnp.float32)
    lsend[0, 1] = jnp.zeros((8, LANES), jnp.float32)
    for side in range(2):
        ssend[side, 0:1] = listed_nodes(eta_ref[...], side)
        ssend[side, 1:2] = listed_nodes(wet_nodes, side)

    pl.semaphore_wait(barrier, count)
    for d in (1, n_z - 1):
        pl.semaphore_signal(tok.at[0], inc=1, device_id=(z_peer(d), g), device_id_type=MESH)
    send_velocity(0)
    send_density(0)
    copy(ssend.at[0], srecv.at[1], ssem, 0, down, g).start()
    copy(ssend.at[1], srecv.at[0], ssem, 0, up, g).start()

    for k in range(K):
        for d in range(TILES):
            cols = slice(d * LANES, (d + 1) * LANES)
            row = slice(d, d + 1)
            nbc[k, row] = nb_ref[k : k + 1, cols]
            wts[0, k, row] = grad_ref[0, k : k + 1, cols]
            wts[1, k, row] = grad_ref[1, k : k + 1, cols]
            wts[2, k, row] = lap_ref[k : k + 1, cols]
        tile = nbc[k] >> 7
        below = jnp.where(p > 0, 1.0, 0.0)
        above = jnp.where(p < n_space - 1, 1.0, 0.0)
        valid = jnp.where(tile == TILES, below, jnp.where(tile == TILES + 1, above, 1.0))
        for j in range(3):
            wts[j, k] = wts[j, k] * valid

    def slots(k, d):
        row = wide(nbc[k, d : d + 1])
        return row & (LANES - 1), row >> 7

    def gather_own():
        for d in range(TILES):
            for k in range(K):
                idx, tile = slots(k, d)
                masks = [tile == t for t in range(TILES)]
                for f in range(4):
                    src = [x[f, t] if f < 3 else ploc[t] for t in range(TILES)]
                    out = lane_gather(src[0], idx)
                    for t in range(1, TILES):
                        out = jnp.where(masks[t], lane_gather(src[t], idx), out)
                    near[f, d * K + k] = out

    def level_terms(s):
        arrived(urecv.at[s], usem, s)
        arrived(rrecv.at[s], rsem, s)
        halo = []
        for side in range(2):
            r = rrecv[s, side]
            halo.append([urecv[s, side, 0], urecv[s, side, 1], r, column(r)[0]])
        for d in range(TILES):
            own = [x[0, d], x[1, d], x[2, d], ploc[d]]
            zero = jnp.zeros((8, LANES), jnp.float32)
            dxu, dyv, lu, lv, lr, dxr, dyr, dxp, dyp = [zero] * 9
            for k in range(K):
                idx, tile = slots(k, d)
                m0, m1 = tile == TILES, tile == TILES + 1
                diff = []
                for f in range(4):
                    n = near[f, d * K + k]
                    n = jnp.where(m0, lane_gather(halo[0][f], idx), n)
                    n = jnp.where(m1, lane_gather(halo[1][f], idx), n)
                    diff.append(n - own[f])
                we, wn, wl = [wide(wts[j, k, d : d + 1]) for j in range(3)]
                dxu += we * diff[0]
                dyv += wn * diff[1]
                lu += wl * diff[0]
                lv += wl * diff[1]
                lr += wl * diff[2]
                dxr += we * diff[2]
                dyr += wn * diff[2]
                dxp += we * diff[3]
                dyp += wn * diff[3]
            u, v, r, _ = own
            cor = wide(cor_ref[d : d + 1])
            drag = jnp.where(level_id == wide(bot_ref[d : d + 1]) - 1, DRAG, 0.0)
            part[0, d] = u + DT * (cor * v - dxp + lu - drag * u)
            part[1, d] = v + DT * (lv - dyp - cor * u - drag * v)
            x[2, d] = r + DT * (lr - u * dxr - v * dyr)
            lsend[s + 1, 1, d : d + 1] = jnp.sum(th * (dxu + dyv), axis=0, keepdims=True)

    def shared_terms(s):
        arrived(lrecv.at[s], lsem, s)
        arrived(grecv.at[s], gsem, s)
        div, mass = lsend[s, 1], jnp.zeros((8, LANES), jnp.float32)
        for d in range(1, n_level):
            mass = mass + jnp.where(g >= d, lrecv[s, d - 1, 0], 0.0)
            div = div + lrecv[s, d - 1, 1]
        spread = wet_nodes * div
        new_eta = eta[...] - DT * spread
        eta[...] = new_eta
        vv[s] = area_ref[...] * spread
        own = new_eta + BUOYANCY * mass
        q[0:8] = own
        for side in range(2):
            row = slice(side, side + 1)
            m = jnp.zeros((1, LANES), jnp.float32)
            h = grecv[s, side, 0, 1:2]
            for d in range(1, n_level):
                m = m + jnp.where(g >= d, grecv[s, side, d, 0:1], 0.0)
                h = h + grecv[s, side, d, 1:2]
            e = etah[row] - DT * srecv[side, 1:2] * h
            etah[row] = e
            q[8 + side : 9 + side] = e + BUOYANCY * m
        dx = jnp.zeros((8, LANES), jnp.float32)
        dy = dx
        rows = [wide(q[t : t + 1]) for t in range(TILES + 2)]
        for k in range(K):
            slot = nbc[k]
            idx, tile = slot & (LANES - 1), slot >> 7
            n = lane_gather(rows[0], idx)
            for t in range(1, TILES + 2):
                n = jnp.where(tile == t, lane_gather(rows[t], idx), n)
            diff = n - own
            dx = dx + wts[0, k] * diff
            dy = dy + wts[1, k] * diff
        dq[0] = DT * dx
        dq[1] = DT * dy
        for d in range(TILES):
            wet = level_id < wide(bot_ref[d : d + 1])
            for c in range(2):
                x[c, d] = jnp.where(wet, part[c, d] - wide(dq[c, d : d + 1]), 0.0)

    def pass_token(i, dist):
        pl.semaphore_wait(tok.at[i - 1], 2)
        for d in (dist, n_z - dist):
            pl.semaphore_signal(tok.at[i], inc=1, device_id=(z_peer(d), g), device_id_type=MESH)

    def step(s, _):
        gather_own()

        @pl.when(s == 0)
        def _():
            arrived(srecv, ssem, 0)
            etah[...] = srecv[:, 0]

        level_terms(s)
        send_density(s + 1)
        shared_terms(s)
        send_velocity(s + 1)

        @pl.when(s == 0)
        def _():
            pass_token(1, 2)

        @pl.when(s == 1)
        def _():
            pass_token(2, 4)

        return 0

    lax.fori_loop(0, STEPS - 1, step, 0)
    last = STEPS - 1
    gather_own()
    level_terms(last)
    lsend[STEPS, 0] = jnp.zeros((8, LANES), jnp.float32)
    send_level(STEPS)
    for d in range(TILES):
        rho_out[:, d * LANES : (d + 1) * LANES] = x[2, d]
    shared_terms(last)
    for d in range(TILES):
        for c in range(2):
            vel_out[c, :, d * LANES : (d + 1) * LANES] = x[c, d]

    arrived(lrecv.at[STEPS], lsem, STEPS)
    div = lsend[STEPS, 1]
    for d in range(1, n_level):
        div = div + lrecv[STEPS, d - 1, 1]
    spread = wet_nodes * div
    sums = jnp.zeros((8, LANES), jnp.float32)
    terms = [vv[s + 1] for s in range(STEPS - 1)]
    terms += [area_ref[...] * spread, area_ref[...] * wet_nodes]
    for j, term in enumerate(terms):
        sums = jnp.where(sub == j, wide(jnp.sum(term, axis=0, keepdims=True)), sums)
    sums = jnp.broadcast_to(jnp.sum(sums, axis=1, keepdims=True), (8, LANES))
    row = jnp.sum(jnp.where(sub == lane, sums, 0.0), axis=0, keepdims=True)
    zsend[...] = row
    pl.semaphore_wait(tok.at[2], 2)
    for d in range(1, n_z):
        copy(zsend, zrecv.at[d - 1], zsem, 0, z_peer(d), g).start()
    arrived(zrecv, zsem, 0)
    for d in range(1, n_z):
        row = row + zrecv[d - 1]
    xsend[...] = row
    for d in range(1, X_CHIPS):
        copy(xsend, xrecv.at[d - 1], zsem, 1, x_peer(d), g).start()
    arrived(xrecv, zsem, 1)
    for d in range(1, X_CHIPS):
        row = row + xrecv[d - 1]
    lane_row = lane[0:1]
    total = jnp.sum(jnp.where(lane_row == STEPS, row, 0.0), axis=1, keepdims=True)
    drifts = jnp.where(lane_row < STEPS, row / total, 0.0)
    drift_out[...] = drifts
    eta_out[...] = eta[...] - DT * spread + DT * jnp.sum(drifts, axis=1, keepdims=True)

    for s in range(STEPS + 1):
        left(lrecv.at[s], lsem, s)
    for s in range(STEPS):
        left(usend.at[s], usem, s)
        left(rsend.at[s], rsem, s)
        left(grecv.at[s], gsem, s)
    left(ssend, ssem, 0)
    left(zrecv, zsem, 0)
    left(xrecv, zsem, 1)


def solution(mesh):
    n_space, n_level = mesh.shape["space"], mesh.shape["level"]

    def local(
        velocity,
        density,
        elevation,
        grad_weights,
        lap_weights,
        coriolis,
        node_area,
        thickness,
        send_list,
        neighbours,
        bottom,
    ):
        f32, i32 = jnp.float32, jnp.int32
        compact = (TILES, LANES)
        vmem = pl.BlockSpec(memory_space=pltpu.VMEM)
        smem = pl.BlockSpec(memory_space=pltpu.SMEM)
        dma = pltpu.SemaphoreType.DMA
        peers = n_level - 1
        n_z = n_space // X_CHIPS
        shapes = [
            ((K, 8, LANES), i32),
            ((3, K, 8, LANES), f32),
            ((3, 8, 8, LANES), f32),
            ((10, 8, LANES), f32),
            ((2, 8, 8, LANES), f32),
            ((4, 48, 8, LANES), f32),
            ((16, LANES), f32),
            ((2, 8, LANES), f32),
            ((8, LANES), f32),
            ((2, LANES), f32),
            ((5, 8, LANES), f32),
            ((5, 2, 8, LANES), f32),
            ((5, peers, 2, 8, LANES), f32),
            ((4, 2, 2, 8, LANES), f32),
            ((4, 2, 2, 8, LANES), f32),
            ((4, 2, 8, LANES), f32),
            ((4, 2, 8, LANES), f32),
            ((4, 2, 2, LANES), f32),
            ((4, 2, n_level, 2, LANES), f32),
            ((2, 2, LANES), f32),
            ((2, 2, LANES), f32),
            ((1, LANES), f32),
            ((n_z - 1, 1, LANES), f32),
            ((1, LANES), f32),
            ((X_CHIPS - 1, 1, LANES), f32),
        ]

        def body(*refs):
            kernel(n_space, n_level, *refs)

        vel, rho, eta, drift = pl.pallas_call(
            body,
            out_shape=(
                jax.ShapeDtypeStruct(velocity.shape, f32),
                jax.ShapeDtypeStruct(density.shape, f32),
                jax.ShapeDtypeStruct(compact, f32),
                jax.ShapeDtypeStruct((1, LANES), f32),
            ),
            in_specs=[vmem] * 7 + [smem] + [vmem] * 3,
            out_specs=(vmem,) * 4,
            scratch_shapes=[pltpu.VMEM(a, t) for a, t in shapes]
            + [
                dma((2, 5)),
                dma((2, 4)),
                dma((2, 4)),
                dma((2, 4)),
                dma((2, 1)),
                dma((2, 2)),
                pltpu.SemaphoreType.REGULAR((3,)),
            ],
            compiler_params=pltpu.CompilerParams(collective_id=0, has_side_effects=True),
        )(
            velocity,
            density,
            elevation.reshape(compact),
            grad_weights,
            lap_weights,
            coriolis.reshape(compact),
            node_area.reshape(compact),
            thickness,
            send_list,
            neighbours,
            bottom.reshape(compact),
        )
        return vel, rho, eta.reshape(elevation.shape), drift[0, :STEPS]

    return jax.shard_map(
        local,
        mesh=mesh,
        in_specs=(
            P(None, "level", "space"),
            P("level", "space"),
            P("space"),
            P(None, None, "space"),
            P(None, "space"),
            P("space"),
            P("space"),
            P("level"),
            P("space", None),
            P(None, "space"),
            P("space"),
        ),
        out_specs=(P(None, "level", "space"), P("level", "space"), P("space"), P()),
        check_vma=False,
    )
```

time: 295 us -> 57.5 us (0.19)
  local copies, waits for them, and re-layouts: 134 us -> 5.32 us
  starting transfers between devices: 67.9 us -> 0 us
  Pallas kernels: 0 us -> 51.1 us
  waiting for transfers between devices: 44.6 us -> 0 us
  other arithmetic: 43.2 us -> 0 us
    gather x10 -> x0, local copies, waits for them, and re-layouts: 121 us -> none  [the longest x4 83.6 us: neighbour_terms(): nearby = jnp.take(node_major, neighbours.reshape(-1), axis=0)]
    pallas_call x0 -> x1, Pallas kernels: none -> 51.1 us  [local(): pl.pallas_call(body, out_shape=(jax.ShapeDtypeStruct(velocity.shape, f32)...]
    all_to_all x5 -> x0, starting transfers between devices: 47.1 us -> none  [sent_to_all(): lax.all_to_all(jnp.broadcast_to(array[None], (devices, *array.shape)), ax...]
    all_to_all x5 -> x0, waiting for transfers between devices: 32.6 us -> none  [sent_to_all(): lax.all_to_all(jnp.broadcast_to(array[None], (devices, *array.shape)), ax...]
    ppermute x8 -> x0, starting transfers between devices: 20.8 us -> none  [the longest x4 15.6 us: extended_2(): before = lax.ppermute(last, axis, up)]
    select_n x7 -> x0, other arithmetic: 20.1 us -> none  [the longest x4 18.7 us: neighbour_terms(): nearby = jnp.take(node_major, neighbours.reshape(-1), axis=0)]
    unnamed x5 -> x0, other arithmetic: 12.7 us -> none
    ppermute x8 -> x0, waiting for transfers between devices: 12 us -> none  [the longest x4 12 us: extended_2(): after = lax.ppermute(first, axis, down)]
  transfers between devices with their start and end apart: 13 -> 0, of which waited for: 8 -> 0; matrix products, arithmetic and copies ran while one was open for 13% -> 0% of each run, Pallas kernels for 0% -> 0%
where the time goes in v1:
time: 57.5 us; the launch traced here: 57 us
  Pallas kernels  51.1 us (89%)
  local copies, waits for them, and re-layouts  5.32 us (9%)
  between operations  0.65 us (1%)
    pallas_call x1, Pallas kernels, local(): pl.pallas_call(body, out_shape=(jax.ShapeDtypeStruct(velocity.shape, f32)...  51.1 us
    unnamed x10, local copies, waits for them, and re-layouts  4.81 us

profile of v1, /device:TPU:1, one launch (start us, length us, event | category | flops | bytes accessed | tf_op | source)
XLA Modules:
  0.0 57.0 jit_solution(7792053124976078086)
XLA Ops:
  0.6 1.4 %copy.15.refs_3_ = f32[2,6,1024]{2,1,0:T(8,128)} copy(f32[2,6,1024]{2,0,1:T(2,128)} %param.14) | data formatting | bytes 98304 | tf_op args[3]
  2.1 51.1 %shard_map.138 = (f32[2,8,1024]{2,1,0:T(8,128)}, f32[8,1024]{1,0:T(8,128)}, f32[8,128]{1,0:T(8,128)}, f32[1,128]{1,0:T(1,128)}) custom-call(f32[2,8,1024]{2,1,0:T(8,128)} %refs_0_.1, f32[8,1024]{1,0:T(8,128)} %refs_1_.1, f32[8,128]{1,0:T(8,128)} %bitcast.7, f32[2,6,1024]{2,1,0:T(8,128)} %copy.15.refs_3_, f32[6,1024]{1,0:T(8,128)} %refs_4_.1, ...), custom_call_target="tpu_custom_call" | custom-call | tf_op jit(solution)/shard_map/pallas_call | solution.py:462
  53.1 0.0 copy-start.2
  53.2 0.6 %copy-done.2 = f32[1,128]{1,0:T(1,128)S(1)} copy-done((f32[1,128]{1,0:T(1,128)S(1)}, f32[1,128]{1,0:T(1,128)}, u32[]{:S(2)}) %copy-start.2) | copy-done | bytes 536
  53.8 0.5 slice_bitcast_fusion
  54.3 0.0 copy-start
  54.3 1.5 %copy.19 = f32[2,8,1024]{2,1,0:T(8,128)} copy(f32[2,8,1024]{2,1,0:T(8,128)} %get-tuple-element.16) | data formatting | bytes 131072
  55.8 0.0 copy-done
  55.8 0.0 copy-start.1
  55.8 0.6 %copy.20 = f32[8,1024]{1,0:T(8,128)} copy(f32[8,1024]{1,0:T(8,128)S(1)} %copy-done) | data formatting | bytes 65536
  56.4 0.1 copy-done.1
  56.4 0.6 %copy.21 = f32[1024]{0:T(1024)} copy(f32[1024]{0:T(1024)S(1)} %bitcast.11) | data formatting | bytes 8192
Async XLA Ops:
  53.1 0.6 %copy-start.2 = (f32[1,128]{1,0:T(1,128)S(1)}, f32[1,128]{1,0:T(1,128)}, u32[]{:S(2)}) copy-start(f32[1,128]{1,0:T(1,128)} %get-tuple-element.11) | copy-start | bytes 1540
  54.3 1.5 %copy-start = (f32[8,1024]{1,0:T(8,128)S(1)}, f32[8,1024]{1,0:T(8,128)}, u32[]{:S(2)}) copy-start(f32[8,1024]{1,0:T(8,128)} %get-tuple-element.17) | copy-start | bytes 98308
  55.8 0.7 %copy-start.1 = (f32[8,128]{1,0:T(8,128)S(1)}, f32[8,128]{1,0:T(8,128)}, u32[]{:S(2)}) copy-start(f32[8,128]{1,0:T(8,128)} %get-tuple-element.10) | copy-start | bytes 12292

commit v2 on v1

--- a/solution.py
+++ b/solution.py
@@ -37,6 +37,21 @@
 def kernel(
     n_space,
     n_level,
+    vel_hbm,
+    rho_hbm,
+    eta_hbm,
+    grad_hbm,
+    lap_hbm,
+    cor_hbm,
+    area_hbm,
+    thick_hbm,
+    send_hbm,
+    nb_hbm,
+    bot_hbm,
+    vel_out,
+    rho_out,
+    eta_out,
+    drift_out,
     vel_ref,
     rho_ref,
     eta_ref,
@@ -48,13 +63,11 @@
     send_ref,
     nb_ref,
     bot_ref,
-    vel_out,
-    rho_out,
-    eta_out,
-    drift_out,
+    isem,
     nbc,
     wts,
     x,
+    r,
     ploc,
     part,
     near,
@@ -96,9 +109,8 @@
         return lax.rem(p + d * X_CHIPS, n_space)
 
     px = lax.rem(p, X_CHIPS)
-
-    def x_peer(d):
-        return p - px + lax.rem(px + d, X_CHIPS)
+    x_peers = [p - px + lax.rem(px + d, X_CHIPS) for d in range(X_CHIPS)]
+    plane = [(a, b) for a in range(X_CHIPS) for b in range(n_level) if a or b]
 
     barrier = pltpu.get_barrier_semaphore()
     count = 0
@@ -110,22 +122,38 @@
         greet(up, level_peers[d])
         greet(down, level_peers[d])
         count += 2
-        if d:
-            greet(p, level_peers[d])
-            count += 1
+    for a, b in plane:
+        greet(x_peers[a], level_peers[b])
+        count += 1
     for d in (1, n_z - 1):
         greet(z_peer(d), g)
         count += 1
-    for d in range(1, X_CHIPS):
-        greet(x_peer(d), g)
-        count += 1
+
+    inputs = [
+        (send_hbm, send_ref),
+        (vel_hbm, vel_ref),
+        (bot_hbm, bot_ref),
+        (rho_hbm, rho_ref),
+        (thick_hbm, thick_ref),
+        (eta_hbm, eta_ref),
+        (nb_hbm, nb_ref),
+        (grad_hbm, grad_ref),
+        (lap_hbm, lap_ref),
+        (cor_hbm, cor_ref),
+        (area_hbm, area_ref),
+    ]
+    loads = [pltpu.make_async_copy(a, b, isem.at[i]) for i, (a, b) in enumerate(inputs)]
+    for load in loads:
+        load.start()
 
     sub = lax.broadcasted_iota(jnp.int32, (8, LANES), 0)
     lane = lax.broadcasted_iota(jnp.int32, (8, LANES), 1)
+    level_id = sub + g * 8
+    for load in loads[:5]:
+        load.wait()
     th = jnp.zeros((8, LANES), jnp.float32)
     for l in range(8):
         th = jnp.where(sub == l, thick_ref[l], th)
-    level_id = sub + g * 8
     send_idx = [send_ref[:, side * LANES : (side + 1) * LANES] for side in range(2)]
     send_lane = [wide(i & (LANES - 1)) for i in send_idx]
     send_tile = [wide(i >> 7) for i in send_idx]
@@ -163,28 +191,32 @@
     def left(buf, sems, i):
         pltpu.make_async_copy(buf, buf, sems.at[0, i]).wait()
 
-    def send_velocity(s):
+    def list_velocity(s):
         for side in range(2):
             for c in range(2):
                 usend[s, side, c] = listed_levels([x[c, d] for d in range(TILES)], side)
+
+    def send_velocity(s):
         copy(usend.at[s, 0], urecv.at[s, 1], usem, s, down, g).start()
         copy(usend.at[s, 1], urecv.at[s, 0], usem, s, up, g).start()
 
-    def send_density(s):
-        tiles = [x[2, d] for d in range(TILES)]
+    def list_density(s, par):
+        tiles = [r[par, d] for d in range(TILES)]
         for side in range(2):
             got = listed_levels(tiles, side)
             rsend[s, side] = got
             gsend[s, side, 0:1] = jnp.sum(got * th, axis=0, keepdims=True)
-            gsend[s, side, 1:2] = listed_nodes(lsend[s, 1], side)
+        for d in range(TILES):
+            ploc[d], lsend[s, 0, d : d + 1] = column(tiles[d])
+
+    def send_density(s):
         copy(rsend.at[s, 0], rrecv.at[s, 1], rsem, s, down, g).start()
         copy(rsend.at[s, 1], rrecv.at[s, 0], rsem, s, up, g).start()
+
+    def send_sums(s):
         for d in range(n_level):
             copy(gsend.at[s, 0], grecv.at[s, 1, d], gsem, s, down, level_peers[d]).start()
             copy(gsend.at[s, 1], grecv.at[s, 0, d], gsem, s, up, level_peers[d]).start()
-        for d in range(TILES):
-            ploc[d], lsend[s, 0, d : d + 1] = column(tiles[d])
-        send_level(s)
 
     def send_level(s):
         for d in range(1, n_level):
@@ -195,29 +227,38 @@
         wet = level_id < wide(bot_ref[d : d + 1])
         for c in range(2):
             x[c, d] = jnp.where(wet, vel_ref[c, :, cols], 0.0)
-        x[2, d] = rho_ref[:, cols]
+        r[0, d] = rho_ref[:, cols]
+    list_velocity(0)
+    list_density(0, 0)
+    lsend[0, 1] = jnp.zeros((8, LANES), jnp.float32)
+    for side in range(2):
+        gsend[0, side, 1:2] = jnp.zeros((1, LANES), jnp.float32)
+    loads[5].wait()
+    wet_nodes = (bot_ref[...] > 0).astype(jnp.float32)
     eta[...] = eta_ref[...]
-    wet_nodes = (bot_ref[...] > 0).astype(jnp.float32)
-    lsend[0, 1] = jnp.zeros((8, LANES), jnp.float32)
     for side in range(2):
         ssend[side, 0:1] = listed_nodes(eta_ref[...], side)
         ssend[side, 1:2] = listed_nodes(wet_nodes, side)
 
     pl.semaphore_wait(barrier, count)
+    send_velocity(0)
+    send_sums(0)
+    send_density(0)
+    send_level(0)
+    copy(ssend.at[0], srecv.at[1], ssem, 0, down, g).start()
+    copy(ssend.at[1], srecv.at[0], ssem, 0, up, g).start()
     for d in (1, n_z - 1):
         pl.semaphore_signal(tok.at[0], inc=1, device_id=(z_peer(d), g), device_id_type=MESH)
-    send_velocity(0)
-    send_density(0)
-    copy(ssend.at[0], srecv.at[1], ssem, 0, down, g).start()
-    copy(ssend.at[1], srecv.at[0], ssem, 0, up, g).start()
-
+
+    for load in loads[6:]:
+        load.wait()
     for k in range(K):
         for d in range(TILES):
             cols = slice(d * LANES, (d + 1) * LANES)
             row = slice(d, d + 1)
             nbc[k, row] = nb_ref[k : k + 1, cols]
-            wts[0, k, row] = grad_ref[0, k : k + 1, cols]
-            wts[1, k, row] = grad_ref[1, k : k + 1, cols]
+            wts[0, k, row] = grad_ref[k, 0:1, cols]
+            wts[1, k, row] = grad_ref[k, 1:2, cols]
             wts[2, k, row] = lap_ref[k : k + 1, cols]
         tile = nbc[k] >> 7
         below = jnp.where(p > 0, 1.0, 0.0)
@@ -230,55 +271,76 @@
         row = wide(nbc[k, d : d + 1])
         return row & (LANES - 1), row >> 7
 
-    def gather_own():
+    def weights(k, d):
+        return [wide(wts[j, k, d : d + 1]) for j in range(3)]
+
+    def gather_velocity():
         for d in range(TILES):
             for k in range(K):
                 idx, tile = slots(k, d)
-                masks = [tile == t for t in range(TILES)]
-                for f in range(4):
-                    src = [x[f, t] if f < 3 else ploc[t] for t in range(TILES)]
-                    out = lane_gather(src[0], idx)
-                    for t in range(1, TILES):
-                        out = jnp.where(masks[t], lane_gather(src[t], idx), out)
-                    near[f, d * K + k] = out
-
-    def level_terms(s):
-        arrived(urecv.at[s], usem, s)
+                outs = [lane_gather(x[c, 0], idx) for c in range(2)]
+                for t in range(1, TILES):
+                    hit = tile == t
+                    outs = [jnp.where(hit, lane_gather(x[c, t], idx), outs[c]) for c in range(2)]
+                for c in range(2):
+                    near[c, d * K + k] = outs[c]
+
+    def density_terms(s, par):
         arrived(rrecv.at[s], rsem, s)
-        halo = []
-        for side in range(2):
-            r = rrecv[s, side]
-            halo.append([urecv[s, side, 0], urecv[s, side, 1], r, column(r)[0]])
+        halo = [(rrecv[s, side], column(rrecv[s, side])[0]) for side in range(2)]
         for d in range(TILES):
-            own = [x[0, d], x[1, d], x[2, d], ploc[d]]
+            own = (r[par, d], ploc[d])
             zero = jnp.zeros((8, LANES), jnp.float32)
-            dxu, dyv, lu, lv, lr, dxr, dyr, dxp, dyp = [zero] * 9
+            lr, dxr, dyr, dxp, dyp = [zero] * 5
             for k in range(K):
                 idx, tile = slots(k, d)
-                m0, m1 = tile == TILES, tile == TILES + 1
-                diff = []
-                for f in range(4):
-                    n = near[f, d * K + k]
-                    n = jnp.where(m0, lane_gather(halo[0][f], idx), n)
-                    n = jnp.where(m1, lane_gather(halo[1][f], idx), n)
-                    diff.append(n - own[f])
-                we, wn, wl = [wide(wts[j, k, d : d + 1]) for j in range(3)]
-                dxu += we * diff[0]
-                dyv += wn * diff[1]
-                lu += wl * diff[0]
-                lv += wl * diff[1]
-                lr += wl * diff[2]
-                dxr += we * diff[2]
-                dyr += wn * diff[2]
-                dxp += we * diff[3]
-                dyp += wn * diff[3]
-            u, v, r, _ = own
+                outs = [lane_gather(r[par, 0], idx), lane_gather(ploc[0], idx)]
+                for t in range(1, TILES + 2):
+                    hit = tile == t
+                    src = (r[par, t], ploc[t]) if t < TILES else halo[t - TILES]
+                    outs = [jnp.where(hit, lane_gather(a, idx), o) for a, o in zip(src, outs)]
+                dr, dp = [a - b for a, b in zip(outs, own)]
+                we, wn, wl = weights(k, d)
+                lr += wl * dr
+                dxr += we * dr
+                dyr += wn * dr
+                dxp += we * dp
+                dyp += wn * dp
+            u, v = x[0, d], x[1, d]
             cor = wide(cor_ref[d : d + 1])
             drag = jnp.where(level_id == wide(bot_ref[d : d + 1]) - 1, DRAG, 0.0)
-            part[0, d] = u + DT * (cor * v - dxp + lu - drag * u)
-            part[1, d] = v + DT * (lv - dyp - cor * u - drag * v)
-            x[2, d] = r + DT * (lr - u * dxr - v * dyr)
+            part[0, d] = u + DT * (cor * v - dxp - drag * u)
+            part[1, d] = v - DT * (cor * u + dyp + drag * v)
+            r[1 - par, d] = own[0] + DT * (lr - u * dxr - v * dyr)
+
+    def velocity_terms(s):
+        arrived(urecv.at[s], usem, s)
+        halo = [[urecv[s, side, c] for c in range(2)] for side in range(2)]
+        for d in range(TILES):
+            u, v = x[0, d], x[1, d]
+            zero = jnp.zeros((8, LANES), jnp.float32)
+            dxu, dyv, lu, lv = [zero] * 4
+            for k in range(K):
+                idx, tile = slots(k, d)
+                outs = [near[c, d * K + k] for c in range(2)]
+                for side in range(2):
+                    hit = tile == TILES + side
+                    outs = [jnp.where(hit, lane_gather(halo[side][c], idx), outs[c]) for c in range(2)]
+                we, wn, wl = weights(k, d)
+                du, dv = outs[0] - u, outs[1] - v
+                dxu += we * du
+                dyv += wn * dv
+                lu += wl * du
+                lv += wl * dv
+            part[0, d] = part[0, d] + DT * lu
+            part[1, d] = part[1, d] + DT * lv
             lsend[s + 1, 1, d : d + 1] = jnp.sum(th * (dxu + dyv), axis=0, keepdims=True)
+        vv[s] = area_ref[...] * wet_nodes * lsend[s + 1, 1]
+
+    def list_divergence(s):
+        div = lsend[s, 1]
+        for side in range(2):
+            gsend[s, side, 1:2] = listed_nodes(div, side)
 
     def shared_terms(s):
         arrived(lrecv.at[s], lsem, s)
@@ -287,10 +349,8 @@
         for d in range(1, n_level):
             mass = mass + jnp.where(g >= d, lrecv[s, d - 1, 0], 0.0)
             div = div + lrecv[s, d - 1, 1]
-        spread = wet_nodes * div
-        new_eta = eta[...] - DT * spread
+        new_eta = eta[...] - DT * wet_nodes * div
         eta[...] = new_eta
-        vv[s] = area_ref[...] * spread
         own = new_eta + BUOYANCY * mass
         q[0:8] = own
         for side in range(2):
@@ -328,16 +388,23 @@
             pl.semaphore_signal(tok.at[i], inc=1, device_id=(z_peer(d), g), device_id_type=MESH)
 
     def step(s, _):
-        gather_own()
+        par = lax.rem(s, 2)
+        gather_velocity()
+        density_terms(s, par)
+        list_density(s + 1, 1 - par)
+        send_density(s + 1)
+        velocity_terms(s)
+        list_divergence(s + 1)
+        send_sums(s + 1)
+        send_level(s + 1)
 
         @pl.when(s == 0)
         def _():
             arrived(srecv, ssem, 0)
             etah[...] = srecv[:, 0]
 
-        level_terms(s)
-        send_density(s + 1)
         shared_terms(s)
+        list_velocity(s + 1)
         send_velocity(s + 1)
 
         @pl.when(s == 0)
@@ -352,25 +419,16 @@
 
     lax.fori_loop(0, STEPS - 1, step, 0)
     last = STEPS - 1
-    gather_own()
-    level_terms(last)
+    par = last % 2
+    gather_velocity()
+    density_terms(last, par)
+    for d in range(TILES):
+        rho_out[:, d * LANES : (d + 1) * LANES] = r[1 - par, d]
     lsend[STEPS, 0] = jnp.zeros((8, LANES), jnp.float32)
-    send_level(STEPS)
-    for d in range(TILES):
-        rho_out[:, d * LANES : (d + 1) * LANES] = x[2, d]
-    shared_terms(last)
-    for d in range(TILES):
-        for c in range(2):
-            vel_out[c, :, d * LANES : (d + 1) * LANES] = x[c, d]
-
-    arrived(lrecv.at[STEPS], lsem, STEPS)
-    div = lsend[STEPS, 1]
-    for d in range(1, n_level):
-        div = div + lrecv[STEPS, d - 1, 1]
-    spread = wet_nodes * div
+    velocity_terms(last)
+
     sums = jnp.zeros((8, LANES), jnp.float32)
-    terms = [vv[s + 1] for s in range(STEPS - 1)]
-    terms += [area_ref[...] * spread, area_ref[...] * wet_nodes]
+    terms = [vv[s] for s in range(STEPS)] + [area_ref[...] * wet_nodes * (1.0 / n_level)]
     for j, term in enumerate(terms):
         sums = jnp.where(sub == j, wide(jnp.sum(term, axis=0, keepdims=True)), sums)
     sums = jnp.broadcast_to(jnp.sum(sums, axis=1, keepdims=True), (8, LANES))
@@ -379,20 +437,32 @@
     pl.semaphore_wait(tok.at[2], 2)
     for d in range(1, n_z):
         copy(zsend, zrecv.at[d - 1], zsem, 0, z_peer(d), g).start()
+    send_level(STEPS)
+
+    shared_terms(last)
+    for d in range(TILES):
+        for c in range(2):
+            vel_out[c, :, d * LANES : (d + 1) * LANES] = x[c, d]
+    arrived(lrecv.at[STEPS], lsem, STEPS)
+    div = lsend[STEPS, 1]
+    for d in range(1, n_level):
+        div = div + lrecv[STEPS, d - 1, 1]
+    eta[...] = eta[...] - DT * wet_nodes * div
+
     arrived(zrecv, zsem, 0)
     for d in range(1, n_z):
         row = row + zrecv[d - 1]
     xsend[...] = row
-    for d in range(1, X_CHIPS):
-        copy(xsend, xrecv.at[d - 1], zsem, 1, x_peer(d), g).start()
+    for i, (a, b) in enumerate(plane):
+        copy(xsend, xrecv.at[i], zsem, 1, x_peers[a], level_peers[b]).start()
     arrived(xrecv, zsem, 1)
-    for d in range(1, X_CHIPS):
-        row = row + xrecv[d - 1]
+    for i in range(len(plane)):
+        row = row + xrecv[i]
     lane_row = lane[0:1]
     total = jnp.sum(jnp.where(lane_row == STEPS, row, 0.0), axis=1, keepdims=True)
     drifts = jnp.where(lane_row < STEPS, row / total, 0.0)
     drift_out[...] = drifts
-    eta_out[...] = eta[...] - DT * spread + DT * jnp.sum(drifts, axis=1, keepdims=True)
+    eta_out[...] = eta[...] + DT * jnp.sum(drifts, axis=1, keepdims=True)
 
     for s in range(STEPS + 1):
         left(lrecv.at[s], lsem, s)
@@ -424,36 +494,51 @@
         f32, i32 = jnp.float32, jnp.int32
         compact = (TILES, LANES)
         vmem = pl.BlockSpec(memory_space=pltpu.VMEM)
-        smem = pl.BlockSpec(memory_space=pltpu.SMEM)
         dma = pltpu.SemaphoreType.DMA
         peers = n_level - 1
         n_z = n_space // X_CHIPS
+        row = (1, LANES)
+        inputs = [
+            pltpu.VMEM(velocity.shape, f32),
+            pltpu.VMEM(density.shape, f32),
+            pltpu.VMEM(compact, f32),
+            pltpu.VMEM((K, 2, TILES * LANES), f32),
+            pltpu.VMEM(lap_weights.shape, f32),
+            pltpu.VMEM(compact, f32),
+            pltpu.VMEM(compact, f32),
+            pltpu.SMEM(thickness.shape, f32),
+            pltpu.VMEM(send_list.shape, i32),
+            pltpu.VMEM(neighbours.shape, i32),
+            pltpu.VMEM(compact, i32),
+            dma((11,)),
+            pltpu.VMEM((K, 8, LANES), i32),
+        ]
         shapes = [
-            ((K, 8, LANES), i32),
-            ((3, K, 8, LANES), f32),
-            ((3, 8, 8, LANES), f32),
-            ((10, 8, LANES), f32),
-            ((2, 8, 8, LANES), f32),
-            ((4, 48, 8, LANES), f32),
-            ((16, LANES), f32),
-            ((2, 8, LANES), f32),
-            ((8, LANES), f32),
-            ((2, LANES), f32),
-            ((5, 8, LANES), f32),
-            ((5, 2, 8, LANES), f32),
-            ((5, peers, 2, 8, LANES), f32),
-            ((4, 2, 2, 8, LANES), f32),
-            ((4, 2, 2, 8, LANES), f32),
-            ((4, 2, 8, LANES), f32),
-            ((4, 2, 8, LANES), f32),
-            ((4, 2, 2, LANES), f32),
-            ((4, 2, n_level, 2, LANES), f32),
-            ((2, 2, LANES), f32),
-            ((2, 2, LANES), f32),
-            ((1, LANES), f32),
-            ((n_z - 1, 1, LANES), f32),
-            ((1, LANES), f32),
-            ((X_CHIPS - 1, 1, LANES), f32),
+            (3, K, 8, LANES),
+            (2, 8, 8, LANES),
+            (2, 8, 8, LANES),
+            (8, 8, LANES),
+            (2, 8, 8, LANES),
+            (2, 48, 8, LANES),
+            (16, LANES),
+            (2, 8, LANES),
+            (8, LANES),
+            (2, LANES),
+            (STEPS, 8, LANES),
+            (STEPS + 1, 2, 8, LANES),
+            (STEPS + 1, peers, 2, 8, LANES),
+            (STEPS, 2, 2, 8, LANES),
+            (STEPS, 2, 2, 8, LANES),
+            (STEPS, 2, 8, LANES),
+            (STEPS, 2, 8, LANES),
+            (STEPS, 2, 2, LANES),
+            (STEPS, 2, n_level, 2, LANES),
+            (2, 2, LANES),
+            (2, 2, LANES),
+            row,
+            (n_z - 1, *row),
+            row,
+            (X_CHIPS * n_level - 1, *row),
         ]
 
         def body(*refs):
@@ -467,9 +552,10 @@
                 jax.ShapeDtypeStruct(compact, f32),
                 jax.ShapeDtypeStruct((1, LANES), f32),
             ),
-            in_specs=[vmem] * 7 + [smem] + [vmem] * 3,
+            in_specs=[pl.BlockSpec(memory_space=pl.ANY)] * 11,
             out_specs=(vmem,) * 4,
-            scratch_shapes=[pltpu.VMEM(a, t) for a, t in shapes]
+            scratch_shapes=inputs
+            + [pltpu.VMEM(shape, f32) for shape in shapes]
             + [
                 dma((2, 5)),
                 dma((2, 4)),
@@ -484,7 +570,7 @@
             velocity,
             density,
             elevation.reshape(compact),
-            grad_weights,
+            jnp.swapaxes(grad_weights, 0, 1),
             lap_weights,
             coriolis.reshape(compact),
             node_area.reshape(compact),

time: 57.5 us -> 55.9 us (0.972)
  local copies, waits for them, and re-layouts: 5.32 us -> 3.87 us
    unnamed x10 -> x9, local copies, waits for them, and re-layouts: 4.81 us -> 3.36 us
where the time goes in v2:
time: 55.9 us; the launch traced here: 55.7 us
  Pallas kernels  51.1 us (91%)
  local copies, waits for them, and re-layouts  3.87 us (7%)
  between operations  0.66 us (1%)
    pallas_call x1, Pallas kernels, local(): pl.pallas_call(body, out_shape=(jax.ShapeDtypeStruct(velocity.shape, f32)...  51.1 us
    unnamed x9, local copies, waits for them, and re-layouts  3.36 us

profile of v2, /device:TPU:1, one launch (start us, length us, event | category | flops | bytes accessed | tf_op | source)
XLA Modules:
  0.0 55.7 jit_solution(8725255697878340372)
XLA Ops:
  0.6 51.1 %shard_map.138 = (f32[2,8,1024]{2,1,0:T(8,128)}, f32[8,1024]{1,0:T(8,128)}, f32[8,128]{1,0:T(8,128)}, f32[1,128]{1,0:T(1,128)}) custom-call(f32[2,8,1024]{2,1,0:T(8,128)} %refs_0_.1, f32[8,1024]{1,0:T(8,128)} %refs_1_.1, f32[8,128]{1,0:T(8,128)} %bitcast.9, f32[6,2,1024]{2,1,0:T(2,128)} %bitcast.8, f32[6,1024]{1,0:T(8,128)} %refs_4_.1, f32[8,128]{1,0:T(8,128)} %bitcast.10, ...), custom_call_target="tpu_custom_call" | custom-call | tf_op jit(solution)/shard_map/pallas_call | solution.py:547
  51.8 0.0 copy-start.2
  51.8 0.6 %copy-done.2 = f32[1,128]{1,0:T(1,128)S(1)} copy-done((f32[1,128]{1,0:T(1,128)S(1)}, f32[1,128]{1,0:T(1,128)}, u32[]{:S(2)}) %copy-start.2) | copy-done | bytes 536
  52.4 0.5 slice_bitcast_fusion
  52.9 0.0 copy-start
  52.9 1.5 %copy.18 = f32[2,8,1024]{2,1,0:T(8,128)} copy(f32[2,8,1024]{2,1,0:T(8,128)} %get-tuple-element.16) | data formatting | bytes 131072
  54.4 0.0 copy-done
  54.4 0.0 copy-start.1
  54.4 0.6 %copy.19 = f32[8,1024]{1,0:T(8,128)} copy(f32[8,1024]{1,0:T(8,128)S(1)} %copy-done) | data formatting | bytes 65536
  55.0 0.1 copy-done.1
  55.1 0.6 %copy.20 = f32[1024]{0:T(1024)} copy(f32[1024]{0:T(1024)S(1)} %bitcast.13) | data formatting | bytes 8192
Async XLA Ops:
  51.8 0.6 %copy-start.2 = (f32[1,128]{1,0:T(1,128)S(1)}, f32[1,128]{1,0:T(1,128)}, u32[]{:S(2)}) copy-start(f32[1,128]{1,0:T(1,128)} %get-tuple-element.11) | copy-start | bytes 1540
  52.9 1.5 %copy-start = (f32[8,1024]{1,0:T(8,128)S(1)}, f32[8,1024]{1,0:T(8,128)}, u32[]{:S(2)}) copy-start(f32[8,1024]{1,0:T(8,128)} %get-tuple-element.17) | copy-start | bytes 98308
  54.4 0.7 %copy-start.1 = (f32[8,128]{1,0:T(8,128)S(1)}, f32[8,128]{1,0:T(8,128)}, u32[]{:S(2)}) copy-start(f32[8,128]{1,0:T(8,128)} %get-tuple-element.10) | copy-start | bytes 12292

commit v3 on v2

--- a/solution.py
+++ b/solution.py
@@ -112,23 +112,6 @@
     x_peers = [p - px + lax.rem(px + d, X_CHIPS) for d in range(X_CHIPS)]
     plane = [(a, b) for a in range(X_CHIPS) for b in range(n_level) if a or b]
 
-    barrier = pltpu.get_barrier_semaphore()
-    count = 0
-
-    def greet(a, b):
-        pl.semaphore_signal(barrier, inc=1, device_id=(a, b), device_id_type=MESH)
-
-    for d in range(n_level):
-        greet(up, level_peers[d])
-        greet(down, level_peers[d])
-        count += 2
-    for a, b in plane:
-        greet(x_peers[a], level_peers[b])
-        count += 1
-    for d in (1, n_z - 1):
-        greet(z_peer(d), g)
-        count += 1
-
     inputs = [
         (send_hbm, send_ref),
         (vel_hbm, vel_ref),
@@ -146,6 +129,20 @@
     for load in loads:
         load.start()
 
+    barrier = pltpu.get_barrier_semaphore()
+    count = 0
+
+    def greet(a, b):
+        pl.semaphore_signal(barrier, inc=1, device_id=(a, b), device_id_type=MESH)
+
+    for d in range(n_level):
+        greet(up, level_peers[d])
+        greet(down, level_peers[d])
+        count += 2
+        if d:
+            greet(p, level_peers[d])
+            count += 1
+
     sub = lax.broadcasted_iota(jnp.int32, (8, LANES), 0)
     lane = lax.broadcasted_iota(jnp.int32, (8, LANES), 1)
     level_id = sub + g * 8
@@ -190,6 +187,15 @@
 
     def left(buf, sems, i):
         pltpu.make_async_copy(buf, buf, sems.at[0, i]).wait()
+
+    def send_token(i):
+        for d in (2**i, n_space - 2**i):
+            there = (lax.rem(p + d, n_space), g)
+            pl.semaphore_signal(tok.at[i], inc=1, device_id=there, device_id_type=MESH)
+
+    def pass_token(i):
+        pl.semaphore_wait(tok.at[i - 1], 2)
+        send_token(i)
 
     def list_velocity(s):
         for side in range(2):
@@ -247,8 +253,7 @@
     send_level(0)
     copy(ssend.at[0], srecv.at[1], ssem, 0, down, g).start()
     copy(ssend.at[1], srecv.at[0], ssem, 0, up, g).start()
-    for d in (1, n_z - 1):
-        pl.semaphore_signal(tok.at[0], inc=1, device_id=(z_peer(d), g), device_id_type=MESH)
+    send_token(0)
 
     for load in loads[6:]:
         load.wait()
@@ -274,32 +279,37 @@
     def weights(k, d):
         return [wide(wts[j, k, d : d + 1]) for j in range(3)]
 
-    def gather_velocity():
+    def gather_own(par):
         for d in range(TILES):
             for k in range(K):
                 idx, tile = slots(k, d)
-                outs = [lane_gather(x[c, 0], idx) for c in range(2)]
-                for t in range(1, TILES):
+                outs = [None] * 4
+                for t in range(TILES):
                     hit = tile == t
-                    outs = [jnp.where(hit, lane_gather(x[c, t], idx), outs[c]) for c in range(2)]
-                for c in range(2):
-                    near[c, d * K + k] = outs[c]
+                    for f, a in enumerate((x[0, t], x[1, t], r[par, t], ploc[t])):
+                        got = lane_gather(a, idx)
+                        outs[f] = jnp.where(hit, got, outs[f]) if t else got
+                for f in range(4):
+                    near[f, d * K + k] = outs[f]
+
+    def with_halo(fields, halo, idx, tile, at):
+        outs = [near[f, at] for f in fields]
+        for side in range(2):
+            hit = tile == TILES + side
+            outs = [jnp.where(hit, lane_gather(a, idx), o) for a, o in zip(halo[side], outs)]
+        return outs
 
     def density_terms(s, par):
         arrived(rrecv.at[s], rsem, s)
         halo = [(rrecv[s, side], column(rrecv[s, side])[0]) for side in range(2)]
         for d in range(TILES):
-            own = (r[par, d], ploc[d])
+            own, own_p = r[par, d], ploc[d]
             zero = jnp.zeros((8, LANES), jnp.float32)
             lr, dxr, dyr, dxp, dyp = [zero] * 5
             for k in range(K):
                 idx, tile = slots(k, d)
-                outs = [lane_gather(r[par, 0], idx), lane_gather(ploc[0], idx)]
-                for t in range(1, TILES + 2):
-                    hit = tile == t
-                    src = (r[par, t], ploc[t]) if t < TILES else halo[t - TILES]
-                    outs = [jnp.where(hit, lane_gather(a, idx), o) for a, o in zip(src, outs)]
-                dr, dp = [a - b for a, b in zip(outs, own)]
+                near_r, near_p = with_halo((2, 3), halo, idx, tile, d * K + k)
+                dr, dp = near_r - own, near_p - own_p
                 we, wn, wl = weights(k, d)
                 lr += wl * dr
                 dxr += we * dr
@@ -311,7 +321,7 @@
             drag = jnp.where(level_id == wide(bot_ref[d : d + 1]) - 1, DRAG, 0.0)
             part[0, d] = u + DT * (cor * v - dxp - drag * u)
             part[1, d] = v - DT * (cor * u + dyp + drag * v)
-            r[1 - par, d] = own[0] + DT * (lr - u * dxr - v * dyr)
+            r[1 - par, d] = own + DT * (lr - u * dxr - v * dyr)
 
     def velocity_terms(s):
         arrived(urecv.at[s], usem, s)
@@ -322,12 +332,9 @@
             dxu, dyv, lu, lv = [zero] * 4
             for k in range(K):
                 idx, tile = slots(k, d)
-                outs = [near[c, d * K + k] for c in range(2)]
-                for side in range(2):
-                    hit = tile == TILES + side
-                    outs = [jnp.where(hit, lane_gather(halo[side][c], idx), outs[c]) for c in range(2)]
+                near_u, near_v = with_halo((0, 1), halo, idx, tile, d * K + k)
                 we, wn, wl = weights(k, d)
-                du, dv = outs[0] - u, outs[1] - v
+                du, dv = near_u - u, near_v - v
                 dxu += we * du
                 dyv += wn * dv
                 lu += wl * du
@@ -382,45 +389,45 @@
             for c in range(2):
                 x[c, d] = jnp.where(wet, part[c, d] - wide(dq[c, d : d + 1]), 0.0)
 
-    def pass_token(i, dist):
-        pl.semaphore_wait(tok.at[i - 1], 2)
-        for d in (dist, n_z - dist):
-            pl.semaphore_signal(tok.at[i], inc=1, device_id=(z_peer(d), g), device_id_type=MESH)
-
     def step(s, _):
         par = lax.rem(s, 2)
-        gather_velocity()
+        gather_own(par)
         density_terms(s, par)
         list_density(s + 1, 1 - par)
         send_density(s + 1)
+
+        @pl.when(s == 0)
+        def _():
+            pass_token(1)
+            arrived(srecv, ssem, 0)
+            etah[...] = srecv[:, 0]
+
+        @pl.when(s == 1)
+        def _():
+            pass_token(3)
+
         velocity_terms(s)
         list_divergence(s + 1)
         send_sums(s + 1)
-        send_level(s + 1)
-
-        @pl.when(s == 0)
-        def _():
-            arrived(srecv, ssem, 0)
-            etah[...] = srecv[:, 0]
-
         shared_terms(s)
         list_velocity(s + 1)
         send_velocity(s + 1)
+        send_level(s + 1)
 
         @pl.when(s == 0)
         def _():
-            pass_token(1, 2)
+            pass_token(2)
 
         @pl.when(s == 1)
         def _():
-            pass_token(2, 4)
+            pass_token(4)
 
         return 0
 
     lax.fori_loop(0, STEPS - 1, step, 0)
     last = STEPS - 1
     par = last % 2
-    gather_velocity()
+    gather_own(par)
     density_terms(last, par)
     for d in range(TILES):
         rho_out[:, d * LANES : (d + 1) * LANES] = r[1 - par, d]
@@ -434,7 +441,7 @@
     sums = jnp.broadcast_to(jnp.sum(sums, axis=1, keepdims=True), (8, LANES))
     row = jnp.sum(jnp.where(sub == lane, sums, 0.0), axis=0, keepdims=True)
     zsend[...] = row
-    pl.semaphore_wait(tok.at[2], 2)
+    pl.semaphore_wait(tok.at[4], 2)
     for d in range(1, n_z):
         copy(zsend, zrecv.at[d - 1], zsem, 0, z_peer(d), g).start()
     send_level(STEPS)
@@ -473,6 +480,18 @@
     left(ssend, ssem, 0)
     left(zrecv, zsem, 0)
     left(xrecv, zsem, 1)
+
+
+def finish(vel, rho, eta, drift, vel_out, rho_out, eta_out, drift_out, sem):
+    copies = [
+        pltpu.make_async_copy(a, b, sem.at[i])
+        for i, (a, b) in enumerate(((vel, vel_out), (rho, rho_out), (eta, eta_out)))
+    ]
+    for c in copies:
+        c.start()
+    drift_out[...] = drift[0, :STEPS]
+    for c in copies:
+        c.wait()
 
 
 def solution(mesh):
@@ -519,7 +538,7 @@
             (2, 8, 8, LANES),
             (8, 8, LANES),
             (2, 8, 8, LANES),
-            (2, 48, 8, LANES),
+            (4, 48, 8, LANES),
             (16, LANES),
             (2, 8, LANES),
             (8, LANES),
@@ -547,10 +566,10 @@
         vel, rho, eta, drift = pl.pallas_call(
             body,
             out_shape=(
-                jax.ShapeDtypeStruct(velocity.shape, f32),
-                jax.ShapeDtypeStruct(density.shape, f32),
-                jax.ShapeDtypeStruct(compact, f32),
-                jax.ShapeDtypeStruct((1, LANES), f32),
+                pltpu.VMEM(velocity.shape, f32),
+                pltpu.VMEM(density.shape, f32),
+                pltpu.VMEM(compact, f32),
+                pltpu.VMEM((1, LANES), f32),
             ),
             in_specs=[pl.BlockSpec(memory_space=pl.ANY)] * 11,
             out_specs=(vmem,) * 4,
@@ -563,7 +582,7 @@
                 dma((2, 4)),
                 dma((2, 1)),
                 dma((2, 2)),
-                pltpu.SemaphoreType.REGULAR((3,)),
+                pltpu.SemaphoreType.REGULAR((5,)),
             ],
             compiler_params=pltpu.CompilerParams(collective_id=0, has_side_effects=True),
         )(
@@ -579,7 +598,20 @@
             neighbours,
             bottom.reshape(compact),
         )
-        return vel, rho, eta.reshape(elevation.shape), drift[0, :STEPS]
+        results = [pltpu.with_memory_space_constraint(a, pltpu.VMEM) for a in (vel, rho, eta, drift)]
+        vel, rho, eta, drift = pl.pallas_call(
+            finish,
+            out_shape=(
+                jax.ShapeDtypeStruct(velocity.shape, f32),
+                jax.ShapeDtypeStruct(density.shape, f32),
+                jax.ShapeDtypeStruct(compact, f32),
+                jax.ShapeDtypeStruct((STEPS,), f32),
+            ),
+            in_specs=[vmem] * 4,
+            out_specs=(pl.BlockSpec(memory_space=pl.ANY),) * 3 + (vmem,),
+            scratch_shapes=[dma((3,))],
+        )(*results)
+        return vel, rho, eta.reshape(elevation.shape), drift
 
     return jax.shard_map(
         local,

time: 55.9 us -> 49.9 us (0.89)
  local copies, waits for them, and re-layouts: 3.87 us -> 0 us
  Pallas kernels: 51.1 us -> 49.1 us
    unnamed x9 -> x0, local copies, waits for them, and re-layouts: 3.36 us -> none
    pallas_call x1 -> x2, Pallas kernels: 51.1 us -> 49.1 us  [the longest x1 47.9 us: local(): pl.pallas_call(body, out_shape=(pltpu.VMEM(velocity.shape, f32), pltpu.VM...]
where the time goes in v3:
time: 49.9 us; the launch traced here: 49.7 us
  Pallas kernels  49.1 us (98%)
  between operations  0.64 us (1%)
    pallas_call x1, Pallas kernels, local(): pl.pallas_call(body, out_shape=(pltpu.VMEM(velocity.shape, f32), pltpu.VM...  47.9 us
    pallas_call x1, Pallas kernels, local(): pl.pallas_call(finish, out_shape=(jax.ShapeDtypeStruct(velocity.shape, f3...  1.18 us

profile of v3, /device:TPU:1, one launch (start us, length us, event | category | flops | bytes accessed | tf_op | source)
XLA Modules:
  0.0 49.7 jit_solution(16456024397534193287)
XLA Ops:
  0.6 47.9 %shard_map.138 = (f32[2,8,1024]{2,1,0:T(8,128)S(1)}, f32[8,1024]{1,0:T(8,128)S(1)}, f32[8,128]{1,0:T(8,128)S(1)}, f32[1,128]{1,0:T(1,128)S(1)}) custom-call(f32[2,8,1024]{2,1,0:T(8,128)} %refs_0_.1, f32[8,1024]{1,0:T(8,128)} %refs_1_.1, f32[8,128]{1,0:T(8,128)} %bitcast.7, f32[6,2,1024]{2,1,0:T(2,128)} %bitcast.6, f32[6,1024]{1,0:T(8,128)} %refs_4_.1, ...), custom_call_target="tpu_custom_call" | custom-call | tf_op jit(solution)/shard_map/pallas_call | solution.py:566
  48.6 1.2 %shard_map.139 = (f32[2,8,1024]{2,1,0:T(8,128)}, f32[8,1024]{1,0:T(8,128)}, f32[8,128]{1,0:T(8,128)}, f32[4]{0:T(128)}) custom-call(f32[2,8,1024]{2,1,0:T(8,128)S(1)} %get-tuple-element.12.vel, f32[8,1024]{1,0:T(8,128)S(1)} %get-tuple-element.13.rho, f32[8,128]{1,0:T(8,128)S(1)} %get-tuple-element.14.eta, f32[1,128]{1,0:T(1,128)S(1)} %get-tuple-element.15.drift), custom_call_target="tpu_custom_call" | custom-call | tf_op jit(solution)/shard_map/pallas_call | solution.py:602

commit v4 on v3

--- a/solution.py
+++ b/solution.py
@@ -68,7 +68,6 @@
     wts,
     x,
     r,
-    ploc,
     part,
     near,
     q,
@@ -90,11 +89,16 @@
     zrecv,
     xsend,
     xrecv,
+    split,
+    coef,
+    bsend,
+    brecv,
     lsem,
     usem,
     rsem,
     gsem,
     ssem,
+    bsem,
     zsem,
     tok,
 ):
@@ -165,12 +169,12 @@
         got = lane_gather(compact, send_lane[side])
         return jnp.sum(jnp.where(send_tile[side] == sub, got, 0.0), axis=0, keepdims=True)
 
-    def column(rho_tile):
-        weighted = rho_tile * th
+    def column(density):
+        weighted = density * th
         total = weighted
         for shift in (1, 2, 4):
             total = total + jnp.where(sub >= shift, pltpu.roll(total, shift, 0), 0.0)
-        return BUOYANCY * (total - 0.5 * weighted), total[7:8]
+        return BUOYANCY * (total - 0.5 * weighted)
 
     def copy(src, dst, sems, i, a, b):
         return pltpu.make_async_remote_copy(
@@ -213,7 +217,7 @@
             rsend[s, side] = got
             gsend[s, side, 0:1] = jnp.sum(got * th, axis=0, keepdims=True)
         for d in range(TILES):
-            ploc[d], lsend[s, 0, d : d + 1] = column(tiles[d])
+            lsend[s, 0, d : d + 1] = jnp.sum(tiles[d] * th, axis=0, keepdims=True)
 
     def send_density(s):
         copy(rsend.at[s, 0], rrecv.at[s, 1], rsem, s, down, g).start()
@@ -283,13 +287,13 @@
         for d in range(TILES):
             for k in range(K):
                 idx, tile = slots(k, d)
-                outs = [None] * 4
+                outs = [None] * 3
                 for t in range(TILES):
                     hit = tile == t
-                    for f, a in enumerate((x[0, t], x[1, t], r[par, t], ploc[t])):
+                    for f, a in enumerate((x[0, t], x[1, t], r[par, t])):
                         got = lane_gather(a, idx)
                         outs[f] = jnp.where(hit, got, outs[f]) if t else got
-                for f in range(4):
+                for f in range(3):
                     near[f, d * K + k] = outs[f]
 
     def with_halo(fields, halo, idx, tile, at):
@@ -301,26 +305,24 @@
 
     def density_terms(s, par):
         arrived(rrecv.at[s], rsem, s)
-        halo = [(rrecv[s, side], column(rrecv[s, side])[0]) for side in range(2)]
+        halo = [(rrecv[s, side],) for side in range(2)]
         for d in range(TILES):
-            own, own_p = r[par, d], ploc[d]
+            own = r[par, d]
             zero = jnp.zeros((8, LANES), jnp.float32)
-            lr, dxr, dyr, dxp, dyp = [zero] * 5
+            lr, dxr, dyr = [zero] * 3
             for k in range(K):
                 idx, tile = slots(k, d)
-                near_r, near_p = with_halo((2, 3), halo, idx, tile, d * K + k)
-                dr, dp = near_r - own, near_p - own_p
+                (near_r,) = with_halo((2,), halo, idx, tile, d * K + k)
+                dr = near_r - own
                 we, wn, wl = weights(k, d)
                 lr += wl * dr
                 dxr += we * dr
                 dyr += wn * dr
-                dxp += we * dp
-                dyp += wn * dp
             u, v = x[0, d], x[1, d]
             cor = wide(cor_ref[d : d + 1])
             drag = jnp.where(level_id == wide(bot_ref[d : d + 1]) - 1, DRAG, 0.0)
-            part[0, d] = u + DT * (cor * v - dxp - drag * u)
-            part[1, d] = v - DT * (cor * u + dyp + drag * v)
+            part[0, d] = u + DT * (cor * v - column(dxr) - drag * u)
+            part[1, d] = v - DT * (cor * u + column(dyr) + drag * v)
             r[1 - par, d] = own + DT * (lr - u * dxr - v * dyr)
 
     def velocity_terms(s):
@@ -389,8 +391,71 @@
             for c in range(2):
                 x[c, d] = jnp.where(wet, part[c, d] - wide(dq[c, d : d + 1]), 0.0)
 
+    def drift_weights():
+        area = area_ref[...] * wet_nodes
+        own = [jnp.zeros((8, LANES), jnp.float32)] * 2
+        for k in range(K):
+            for j in range(2):
+                term = area * wts[j, k]
+                own[j] = own[j] + term
+                for i in range(3):
+                    short = term.astype(jnp.bfloat16).astype(jnp.float32)
+                    split[i, j, k] = short
+                    term = term - short
+        target = jnp.where(sub < 2, sub + TILES, jnp.where(sub < 4, sub + TILES - 2, -1))
+        slot_lane = lax.broadcasted_iota(jnp.int32, (LANES, LANES), 0)
+        total = jnp.zeros((72, LANES), jnp.float32)
+        for k in range(K):
+            for d in range(0, TILES, 2):
+                left_side, right_side = [], []
+                for e in (d, d + 1):
+                    row = nbc[k, e : e + 1]
+                    tile = wide(row >> 7)
+                    hit, far = tile == sub, tile == target
+                    pieces = []
+                    for i in range(3):
+                        we, wn = [wide(split[i, j, k, e : e + 1]) for j in range(2)]
+                        pieces.append(jnp.where(hit, we, 0.0))
+                        pieces.append(jnp.where(hit, wn, 0.0))
+                        pieces.append(jnp.where(far, jnp.where(sub < 2, we, wn), 0.0))
+                    left_side.append(jnp.concatenate(pieces, axis=0))
+                    same = jnp.broadcast_to(row & (LANES - 1), (LANES, LANES)) == slot_lane
+                    right_side.append(jnp.where(same, 1.0, 0.0))
+                total = total + lax.dot_general(
+                    jnp.concatenate(left_side, axis=1).astype(jnp.bfloat16),
+                    jnp.concatenate(right_side, axis=1).astype(jnp.bfloat16),
+                    (((1,), (1,)), ((), ())),
+                    preferred_element_type=jnp.float32,
+                )
+        total = total[0:24] + total[24:48] + total[48:72]
+        for j in range(2):
+            coef[j] = total[8 * j : 8 * j + 8] - own[j]
+            for side in range(2):
+                bsend[side, j : j + 1] = total[16 + 2 * j + side : 17 + 2 * j + side]
+        copy(bsend.at[0], brecv.at[1], bsem, 0, down, g).start()
+        copy(bsend.at[1], brecv.at[0], bsem, 0, up, g).start()
+
+    def early_drift():
+        arrived(brecv, bsem, 0)
+        total = jnp.zeros((8, LANES), jnp.float32)
+        for j in range(2):
+            for d in range(TILES):
+                total = total + wide(coef[j, d : d + 1]) * x[j, d]
+            for side in range(2):
+                total = total + wide(brecv[side, j : j + 1]) * usend[STEPS - 1, side, j]
+        return total * th
+
     def step(s, _):
         par = lax.rem(s, 2)
+        @pl.when(s == 1)
+        def _():
+            pass_token(2)
+            drift_weights()
+
+        @pl.when(s == 2)
+        def _():
+            pass_token(4)
+
         gather_own(par)
         density_terms(s, par)
         list_density(s + 1, 1 - par)
@@ -413,29 +478,15 @@
         list_velocity(s + 1)
         send_velocity(s + 1)
         send_level(s + 1)
-
-        @pl.when(s == 0)
-        def _():
-            pass_token(2)
-
-        @pl.when(s == 1)
-        def _():
-            pass_token(4)
-
         return 0
 
     lax.fori_loop(0, STEPS - 1, step, 0)
     last = STEPS - 1
     par = last % 2
-    gather_own(par)
-    density_terms(last, par)
-    for d in range(TILES):
-        rho_out[:, d * LANES : (d + 1) * LANES] = r[1 - par, d]
-    lsend[STEPS, 0] = jnp.zeros((8, LANES), jnp.float32)
-    velocity_terms(last)
 
     sums = jnp.zeros((8, LANES), jnp.float32)
-    terms = [vv[s] for s in range(STEPS)] + [area_ref[...] * wet_nodes * (1.0 / n_level)]
+    terms = [vv[s] for s in range(last)]
+    terms += [early_drift(), area_ref[...] * wet_nodes * (1.0 / n_level)]
     for j, term in enumerate(terms):
         sums = jnp.where(sub == j, wide(jnp.sum(term, axis=0, keepdims=True)), sums)
     sums = jnp.broadcast_to(jnp.sum(sums, axis=1, keepdims=True), (8, LANES))
@@ -444,17 +495,18 @@
     pl.semaphore_wait(tok.at[4], 2)
     for d in range(1, n_z):
         copy(zsend, zrecv.at[d - 1], zsem, 0, z_peer(d), g).start()
+
+    gather_own(par)
+    density_terms(last, par)
+    for d in range(TILES):
+        rho_out[:, d * LANES : (d + 1) * LANES] = r[1 - par, d]
+    lsend[STEPS, 0] = jnp.zeros((8, LANES), jnp.float32)
+    velocity_terms(last)
     send_level(STEPS)
-
     shared_terms(last)
     for d in range(TILES):
         for c in range(2):
             vel_out[c, :, d * LANES : (d + 1) * LANES] = x[c, d]
-    arrived(lrecv.at[STEPS], lsem, STEPS)
-    div = lsend[STEPS, 1]
-    for d in range(1, n_level):
-        div = div + lrecv[STEPS, d - 1, 1]
-    eta[...] = eta[...] - DT * wet_nodes * div
 
     arrived(zrecv, zsem, 0)
     for d in range(1, n_z):
@@ -462,6 +514,13 @@
     xsend[...] = row
     for i, (a, b) in enumerate(plane):
         copy(xsend, xrecv.at[i], zsem, 1, x_peers[a], level_peers[b]).start()
+
+    arrived(lrecv.at[STEPS], lsem, STEPS)
+    div = lsend[STEPS, 1]
+    for d in range(1, n_level):
+        div = div + lrecv[STEPS, d - 1, 1]
+    eta[...] = eta[...] - DT * wet_nodes * div
+
     arrived(xrecv, zsem, 1)
     for i in range(len(plane)):
         row = row + xrecv[i]
@@ -478,6 +537,7 @@
         left(rsend.at[s], rsem, s)
         left(grecv.at[s], gsem, s)
     left(ssend, ssem, 0)
+    left(bsend, bsem, 0)
     left(zrecv, zsem, 0)
     left(xrecv, zsem, 1)
 
@@ -536,9 +596,8 @@
             (3, K, 8, LANES),
             (2, 8, 8, LANES),
             (2, 8, 8, LANES),
-            (8, 8, LANES),
             (2, 8, 8, LANES),
-            (4, 48, 8, LANES),
+            (3, 48, 8, LANES),
             (16, LANES),
             (2, 8, LANES),
             (8, LANES),
@@ -558,6 +617,10 @@
             (n_z - 1, *row),
             row,
             (X_CHIPS * n_level - 1, *row),
+            (3, 2, K, 8, LANES),
+            (2, 8, LANES),
+            (2, 2, LANES),
+            (2, 2, LANES),
         ]
 
         def body(*refs):
@@ -580,6 +643,7 @@
                 dma((2, 4)),
                 dma((2, 4)),
                 dma((2, 4)),
+                dma((2, 1)),
                 dma((2, 1)),
                 dma((2, 2)),
                 pltpu.SemaphoreType.REGULAR((5,)),

time: 49.9 us -> 46 us (0.922)
  Pallas kernels: 49.1 us -> 45.2 us
    pallas_call x1, Pallas kernels: 47.9 us -> 44 us  [local(): pl.pallas_call(body, out_shape=(pltpu.VMEM(velocity.shape, f32), pltpu.VM...]
where the time goes in v4:
time: 46 us; the launch traced here: 45.8 us
  Pallas kernels  45.2 us (98%)
  between operations  0.64 us (1%)
    pallas_call x1, Pallas kernels, local(): pl.pallas_call(body, out_shape=(pltpu.VMEM(velocity.shape, f32), pltpu.VM...  44 us
    pallas_call x1, Pallas kernels, local(): pl.pallas_call(finish, out_shape=(jax.ShapeDtypeStruct(velocity.shape, f3...  1.18 us

profile of v4, /device:TPU:1, one launch (start us, length us, event | category | flops | bytes accessed | tf_op | source)
XLA Modules:
  0.0 45.8 jit_solution(8167291957212573593)
XLA Ops:
  0.6 44.0 %shard_map.138 = (f32[2,8,1024]{2,1,0:T(8,128)S(1)}, f32[8,1024]{1,0:T(8,128)S(1)}, f32[8,128]{1,0:T(8,128)S(1)}, f32[1,128]{1,0:T(1,128)S(1)}) custom-call(f32[2,8,1024]{2,1,0:T(8,128)} %refs_0_.1, f32[8,1024]{1,0:T(8,128)} %refs_1_.1, f32[8,128]{1,0:T(8,128)} %bitcast.7, f32[6,2,1024]{2,1,0:T(2,128)} %bitcast.6, f32[6,1024]{1,0:T(8,128)} %refs_4_.1, ...), custom_call_target="tpu_custom_call" | custom-call | tf_op jit(solution)/shard_map/pallas_call | solution.py:629
  44.6 1.2 %shard_map.139 = (f32[2,8,1024]{2,1,0:T(8,128)}, f32[8,1024]{1,0:T(8,128)}, f32[8,128]{1,0:T(8,128)}, f32[4]{0:T(128)}) custom-call(f32[2,8,1024]{2,1,0:T(8,128)S(1)} %get-tuple-element.12.vel, f32[8,1024]{1,0:T(8,128)S(1)} %get-tuple-element.13.rho, f32[8,128]{1,0:T(8,128)S(1)} %get-tuple-element.14.eta, f32[1,128]{1,0:T(1,128)S(1)} %get-tuple-element.15.drift), custom_call_target="tpu_custom_call" | custom-call | tf_op jit(solution)/shard_map/pallas_call | solution.py:666

commit v5 on v4

--- a/solution.py
+++ b/solution.py
@@ -28,6 +28,10 @@
     return lax.gather(
         x, idx[..., None], _LANE_GATHER, (1, 1), mode=lax.GatherScatterMode.PROMISE_IN_BOUNDS
     )
+
+
+def far_first(count, start=1):
+    return sorted(range(start, count), key=lambda d: -min(d, count - d))
 
 
 def wide(row):
@@ -115,6 +119,21 @@
     px = lax.rem(p, X_CHIPS)
     x_peers = [p - px + lax.rem(px + d, X_CHIPS) for d in range(X_CHIPS)]
     plane = [(a, b) for a in range(X_CHIPS) for b in range(n_level) if a or b]
+    plane.sort(key=lambda ab: -2 * min(ab[0], X_CHIPS - ab[0]) - min(ab[1], n_level - ab[1]))
+
+    barrier = pltpu.get_barrier_semaphore()
+    count = 0
+
+    def greet(a, b):
+        pl.semaphore_signal(barrier, inc=1, device_id=(a, b), device_id_type=MESH)
+
+    for d in far_first(n_level, 0):
+        greet(up, level_peers[d])
+        greet(down, level_peers[d])
+        count += 2
+        if d:
+            greet(p, level_peers[d])
+            count += 1
 
     inputs = [
         (send_hbm, send_ref),
@@ -133,20 +152,6 @@
     for load in loads:
         load.start()
 
-    barrier = pltpu.get_barrier_semaphore()
-    count = 0
-
-    def greet(a, b):
-        pl.semaphore_signal(barrier, inc=1, device_id=(a, b), device_id_type=MESH)
-
-    for d in range(n_level):
-        greet(up, level_peers[d])
-        greet(down, level_peers[d])
-        count += 2
-        if d:
-            greet(p, level_peers[d])
-            count += 1
-
     sub = lax.broadcasted_iota(jnp.int32, (8, LANES), 0)
     lane = lax.broadcasted_iota(jnp.int32, (8, LANES), 1)
     level_id = sub + g * 8
@@ -224,12 +229,12 @@
         copy(rsend.at[s, 1], rrecv.at[s, 0], rsem, s, up, g).start()
 
     def send_sums(s):
-        for d in range(n_level):
+        for d in far_first(n_level, 0):
             copy(gsend.at[s, 0], grecv.at[s, 1, d], gsem, s, down, level_peers[d]).start()
             copy(gsend.at[s, 1], grecv.at[s, 0, d], gsem, s, up, level_peers[d]).start()
 
     def send_level(s):
-        for d in range(1, n_level):
+        for d in far_first(n_level):
             copy(lsend.at[s], lrecv.at[s, d - 1], lsem, s, p, level_peers[d]).start()
 
     for d in range(TILES):
@@ -493,7 +498,7 @@
     row = jnp.sum(jnp.where(sub == lane, sums, 0.0), axis=0, keepdims=True)
     zsend[...] = row
     pl.semaphore_wait(tok.at[4], 2)
-    for d in range(1, n_z):
+    for d in far_first(n_z):
         copy(zsend, zrecv.at[d - 1], zsem, 0, z_peer(d), g).start()
 
     gather_own(par)

time: 46 us -> 45.8 us (level)
  no operation moved by 1% of the time
where the time goes in v5:
time: 45.8 us; the launch traced here: 45.6 us
  Pallas kernels  45 us (98%)
  between operations  0.64 us (1%)
    pallas_call x1, Pallas kernels, local(): pl.pallas_call(body, out_shape=(pltpu.VMEM(velocity.shape, f32), pltpu.VM...  43.8 us
    pallas_call x1, Pallas kernels, local(): pl.pallas_call(finish, out_shape=(jax.ShapeDtypeStruct(velocity.shape, f3...  1.18 us

profile of v5, /device:TPU:1, one launch (start us, length us, event | category | flops | bytes accessed | tf_op | source)
XLA Modules:
  0.0 45.6 jit_solution(13533488121131052513)
XLA Ops:
  0.6 43.8 %shard_map.138 = (f32[2,8,1024]{2,1,0:T(8,128)S(1)}, f32[8,1024]{1,0:T(8,128)S(1)}, f32[8,128]{1,0:T(8,128)S(1)}, f32[1,128]{1,0:T(1,128)S(1)}) custom-call(f32[2,8,1024]{2,1,0:T(8,128)} %refs_0_.1, f32[8,1024]{1,0:T(8,128)} %refs_1_.1, f32[8,128]{1,0:T(8,128)} %bitcast.7, f32[6,2,1024]{2,1,0:T(2,128)} %bitcast.6, f32[6,1024]{1,0:T(8,128)} %refs_4_.1, ...), custom_call_target="tpu_custom_call" | custom-call | tf_op jit(solution)/shard_map/pallas_call | solution.py:634
  44.4 1.2 %shard_map.139 = (f32[2,8,1024]{2,1,0:T(8,128)}, f32[8,1024]{1,0:T(8,128)}, f32[8,128]{1,0:T(8,128)}, f32[4]{0:T(128)}) custom-call(f32[2,8,1024]{2,1,0:T(8,128)S(1)} %get-tuple-element.12.vel, f32[8,1024]{1,0:T(8,128)S(1)} %get-tuple-element.13.rho, f32[8,128]{1,0:T(8,128)S(1)} %get-tuple-element.14.eta, f32[1,128]{1,0:T(1,128)S(1)} %get-tuple-element.15.drift), custom_call_target="tpu_custom_call" | custom-call | tf_op jit(solution)/shard_map/pallas_call | solution.py:671

commit v6 on v5

--- a/solution.py
+++ b/solution.py
@@ -70,6 +70,8 @@
     isem,
     nbc,
     wts,
+    bots,
+    cors,
     x,
     r,
     part,
@@ -172,7 +174,8 @@
 
     def listed_nodes(compact, side):
         got = lane_gather(compact, send_lane[side])
-        return jnp.sum(jnp.where(send_tile[side] == sub, got, 0.0), axis=0, keepdims=True)
+        here = jnp.where(send_tile[side] == sub, got, jnp.zeros_like(got))
+        return jnp.sum(here, axis=0, keepdims=True)
 
     def column(density):
         weighted = density * th
@@ -266,6 +269,8 @@
 
     for load in loads[6:]:
         load.wait()
+    bots[0:8] = bot_ref[...]
+    cors[0:8] = cor_ref[...]
     for k in range(K):
         for d in range(TILES):
             cols = slice(d * LANES, (d + 1) * LANES)
@@ -274,12 +279,24 @@
             wts[0, k, row] = grad_ref[k, 0:1, cols]
             wts[1, k, row] = grad_ref[k, 1:2, cols]
             wts[2, k, row] = lap_ref[k : k + 1, cols]
-        tile = nbc[k] >> 7
+        tile = nbc[k, 0:8] >> 7
         below = jnp.where(p > 0, 1.0, 0.0)
         above = jnp.where(p < n_space - 1, 1.0, 0.0)
         valid = jnp.where(tile == TILES, below, jnp.where(tile == TILES + 1, above, 1.0))
+        nbc[k, 8:16] = jnp.zeros((8, LANES), jnp.int32)
         for j in range(3):
-            wts[j, k] = wts[j, k] * valid
+            wts[j, k, 0:8] = wts[j, k, 0:8] * valid
+            wts[j, k, 8:16] = jnp.zeros((8, LANES), jnp.float32)
+        for side in range(2):
+            row = slice(8 + side, 9 + side)
+            nbc[k, row] = listed_nodes(nbc[k, 0:8], side)
+            for j in range(3):
+                wts[j, k, row] = listed_nodes(wts[j, k, 0:8], side)
+    for side in range(2):
+        row = slice(8 + side, 9 + side)
+        bots[row] = listed_nodes(bot_ref[...], side)
+        cors[row] = listed_nodes(cor_ref[...], side)
+    lists = (TILES, TILES + 1)
 
     def slots(k, d):
         row = wide(nbc[k, d : d + 1])
@@ -288,8 +305,8 @@
     def weights(k, d):
         return [wide(wts[j, k, d : d + 1]) for j in range(3)]
 
-    def gather_own(par):
-        for d in range(TILES):
+    def gather_own(par, dests):
+        for d in dests:
             for k in range(K):
                 idx, tile = slots(k, d)
                 outs = [None] * 3
@@ -308,11 +325,15 @@
             outs = [jnp.where(hit, lane_gather(a, idx), o) for a, o in zip(halo[side], outs)]
         return outs
 
-    def density_terms(s, par):
-        arrived(rrecv.at[s], rsem, s)
+    def velocity_of(s, d):
+        if d >= TILES:
+            return usend[s, d - TILES, 0], usend[s, d - TILES, 1]
+        return x[0, d], x[1, d]
+
+    def density_terms(s, par, dests):
         halo = [(rrecv[s, side],) for side in range(2)]
-        for d in range(TILES):
-            own = r[par, d]
+        for d in dests:
+            own = rsend[s, d - TILES] if d >= TILES else r[par, d]
             zero = jnp.zeros((8, LANES), jnp.float32)
             lr, dxr, dyr = [zero] * 3
             for k in range(K):
@@ -323,18 +344,23 @@
                 lr += wl * dr
                 dxr += we * dr
                 dyr += wn * dr
-            u, v = x[0, d], x[1, d]
-            cor = wide(cor_ref[d : d + 1])
-            drag = jnp.where(level_id == wide(bot_ref[d : d + 1]) - 1, DRAG, 0.0)
+            u, v = velocity_of(s, d)
+            cor = wide(cors[d : d + 1])
+            drag = jnp.where(level_id == wide(bots[d : d + 1]) - 1, DRAG, 0.0)
             part[0, d] = u + DT * (cor * v - column(dxr) - drag * u)
             part[1, d] = v - DT * (cor * u + column(dyr) + drag * v)
-            r[1 - par, d] = own + DT * (lr - u * dxr - v * dyr)
-
-    def velocity_terms(s):
-        arrived(urecv.at[s], usem, s)
+            new = own + DT * (lr - u * dxr - v * dyr)
+            if d >= TILES:
+                rsend[s + 1, d - TILES] = new
+                gsend[s + 1, d - TILES, 0:1] = jnp.sum(new * th, axis=0, keepdims=True)
+            else:
+                r[1 - par, d] = new
+                lsend[s + 1, 0, d : d + 1] = jnp.sum(new * th, axis=0, keepdims=True)
+
+    def velocity_terms(s, dests):
         halo = [[urecv[s, side, c] for c in range(2)] for side in range(2)]
-        for d in range(TILES):
-            u, v = x[0, d], x[1, d]
+        for d in dests:
+            u, v = velocity_of(s, d)
             zero = jnp.zeros((8, LANES), jnp.float32)
             dxu, dyv, lu, lv = [zero] * 4
             for k in range(K):
@@ -348,15 +374,13 @@
                 lv += wl * dv
             part[0, d] = part[0, d] + DT * lu
             part[1, d] = part[1, d] + DT * lv
-            lsend[s + 1, 1, d : d + 1] = jnp.sum(th * (dxu + dyv), axis=0, keepdims=True)
-        vv[s] = area_ref[...] * wet_nodes * lsend[s + 1, 1]
-
-    def list_divergence(s):
-        div = lsend[s, 1]
-        for side in range(2):
-            gsend[s, side, 1:2] = listed_nodes(div, side)
-
-    def shared_terms(s):
+            div = jnp.sum(th * (dxu + dyv), axis=0, keepdims=True)
+            if d >= TILES:
+                gsend[s + 1, d - TILES, 1:2] = div
+            else:
+                lsend[s + 1, 1, d : d + 1] = div
+
+    def find_q(s):
         arrived(lrecv.at[s], lsem, s)
         arrived(grecv.at[s], gsem, s)
         div, mass = lsend[s, 1], jnp.zeros((8, LANES), jnp.float32)
@@ -365,8 +389,7 @@
             div = div + lrecv[s, d - 1, 1]
         new_eta = eta[...] - DT * wet_nodes * div
         eta[...] = new_eta
-        own = new_eta + BUOYANCY * mass
-        q[0:8] = own
+        q[0:8] = new_eta + BUOYANCY * mass
         for side in range(2):
             row = slice(side, side + 1)
             m = jnp.zeros((1, LANES), jnp.float32)
@@ -377,31 +400,39 @@
             e = etah[row] - DT * srecv[side, 1:2] * h
             etah[row] = e
             q[8 + side : 9 + side] = e + BUOYANCY * m
+
+    def shared_terms(dests):
+        listed = dests[0] >= TILES
+        rows = slice(8, 16) if listed else slice(0, 8)
+        own = q[0:8]
+        if listed:
+            first, second = [wide(listed_nodes(own, side)) for side in range(2)]
+            own = jnp.where(sub == 0, first, second)
         dx = jnp.zeros((8, LANES), jnp.float32)
         dy = dx
-        rows = [wide(q[t : t + 1]) for t in range(TILES + 2)]
+        source = [wide(q[t : t + 1]) for t in range(TILES + 2)]
         for k in range(K):
-            slot = nbc[k]
+            slot = nbc[k, rows]
             idx, tile = slot & (LANES - 1), slot >> 7
-            n = lane_gather(rows[0], idx)
+            n = lane_gather(source[0], idx)
             for t in range(1, TILES + 2):
-                n = jnp.where(tile == t, lane_gather(rows[t], idx), n)
+                n = jnp.where(tile == t, lane_gather(source[t], idx), n)
             diff = n - own
-            dx = dx + wts[0, k] * diff
-            dy = dy + wts[1, k] * diff
-        dq[0] = DT * dx
-        dq[1] = DT * dy
-        for d in range(TILES):
-            wet = level_id < wide(bot_ref[d : d + 1])
-            for c in range(2):
-                x[c, d] = jnp.where(wet, part[c, d] - wide(dq[c, d : d + 1]), 0.0)
+            dx = dx + wts[0, k, rows] * diff
+            dy = dy + wts[1, k, rows] * diff
+        dq[0, rows] = DT * dx
+        dq[1, rows] = DT * dy
+
+    def new_velocity(d, c):
+        wet = level_id < wide(bots[d : d + 1])
+        return jnp.where(wet, part[c, d] - wide(dq[c, d : d + 1]), 0.0)
 
     def drift_weights():
         area = area_ref[...] * wet_nodes
         own = [jnp.zeros((8, LANES), jnp.float32)] * 2
         for k in range(K):
             for j in range(2):
-                term = area * wts[j, k]
+                term = area * wts[j, k, 0:8]
                 own[j] = own[j] + term
                 for i in range(3):
                     short = term.astype(jnp.bfloat16).astype(jnp.float32)
@@ -461,10 +492,11 @@
         def _():
             pass_token(4)
 
-        gather_own(par)
-        density_terms(s, par)
-        list_density(s + 1, 1 - par)
+        gather_own(par, (*lists, *range(TILES)))
+        arrived(rrecv.at[s], rsem, s)
+        density_terms(s, par, lists)
         send_density(s + 1)
+        density_terms(s, par, range(TILES))
 
         @pl.when(s == 0)
         def _():
@@ -476,13 +508,22 @@
         def _():
             pass_token(3)
 
-        velocity_terms(s)
-        list_divergence(s + 1)
+        arrived(urecv.at[s], usem, s)
+        velocity_terms(s, lists)
         send_sums(s + 1)
-        shared_terms(s)
-        list_velocity(s + 1)
+        find_q(s)
+        shared_terms(lists)
+        for side in range(2):
+            for c in range(2):
+                usend[s + 1, side, c] = new_velocity(TILES + side, c)
         send_velocity(s + 1)
+        velocity_terms(s, range(TILES))
         send_level(s + 1)
+        vv[s] = area_ref[...] * wet_nodes * lsend[s + 1, 1]
+        shared_terms(range(TILES))
+        for d in range(TILES):
+            for c in range(2):
+                x[c, d] = new_velocity(d, c)
         return 0
 
     lax.fori_loop(0, STEPS - 1, step, 0)
@@ -501,17 +542,19 @@
     for d in far_first(n_z):
         copy(zsend, zrecv.at[d - 1], zsem, 0, z_peer(d), g).start()
 
-    gather_own(par)
-    density_terms(last, par)
+    gather_own(par, range(TILES))
+    arrived(rrecv.at[last], rsem, last)
+    density_terms(last, par, range(TILES))
     for d in range(TILES):
         rho_out[:, d * LANES : (d + 1) * LANES] = r[1 - par, d]
-    lsend[STEPS, 0] = jnp.zeros((8, LANES), jnp.float32)
-    velocity_terms(last)
+    arrived(urecv.at[last], usem, last)
+    velocity_terms(last, range(TILES))
     send_level(STEPS)
-    shared_terms(last)
+    find_q(last)
+    shared_terms(range(TILES))
     for d in range(TILES):
         for c in range(2):
-            vel_out[c, :, d * LANES : (d + 1) * LANES] = x[c, d]
+            vel_out[c, :, d * LANES : (d + 1) * LANES] = new_velocity(d, c)
 
     arrived(zrecv, zsem, 0)
     for d in range(1, n_z):
@@ -595,16 +638,15 @@
             pltpu.VMEM(neighbours.shape, i32),
             pltpu.VMEM(compact, i32),
             dma((11,)),
-            pltpu.VMEM((K, 8, LANES), i32),
+            pltpu.VMEM((K, 16, LANES), i32),
         ]
         shapes = [
-            (3, K, 8, LANES),
             (2, 8, 8, LANES),
             (2, 8, 8, LANES),
-            (2, 8, 8, LANES),
-            (3, 48, 8, LANES),
+            (2, 10, 8, LANES),
+            (3, 60, 8, LANES),
             (16, LANES),
-            (2, 8, LANES),
+            (2, 16, LANES),
             (8, LANES),
             (2, LANES),
             (STEPS, 8, LANES),
@@ -642,6 +684,8 @@
             in_specs=[pl.BlockSpec(memory_space=pl.ANY)] * 11,
             out_specs=(vmem,) * 4,
             scratch_shapes=inputs
+            + [pltpu.VMEM((3, K, 16, LANES), f32)]
+            + [pltpu.VMEM((16, LANES), i32), pltpu.VMEM((16, LANES), f32)]
             + [pltpu.VMEM(shape, f32) for shape in shapes]
             + [
                 dma((2, 5)),

time: 45.8 us -> 45.5 us (level)
  no operation moved by 1% of the time
where the time goes in v6:
time: 45.5 us; the launch traced here: 45.3 us
  Pallas kernels  44.6 us (98%)
  between operations  0.64 us (1%)
    pallas_call x1, Pallas kernels, local(): pl.pallas_call(body, out_shape=(pltpu.VMEM(velocity.shape, f32), pltpu.VM...  43.5 us
    pallas_call x1, Pallas kernels, local(): pl.pallas_call(finish, out_shape=(jax.ShapeDtypeStruct(velocity.shape, f3...  1.18 us

profile of v6, /device:TPU:1, one launch (start us, length us, event | category | flops | bytes accessed | tf_op | source)
XLA Modules:
  0.0 45.3 jit_solution(13659466568193030723)
XLA Ops:
  0.6 43.5 %shard_map.138 = (f32[2,8,1024]{2,1,0:T(8,128)S(1)}, f32[8,1024]{1,0:T(8,128)S(1)}, f32[8,128]{1,0:T(8,128)S(1)}, f32[1,128]{1,0:T(1,128)S(1)}) custom-call(f32[2,8,1024]{2,1,0:T(8,128)} %refs_0_.1, f32[8,1024]{1,0:T(8,128)} %refs_1_.1, f32[8,128]{1,0:T(8,128)} %bitcast.7, f32[6,2,1024]{2,1,0:T(2,128)} %bitcast.6, f32[6,1024]{1,0:T(8,128)} %refs_4_.1, ...), custom_call_target="tpu_custom_call" | custom-call | tf_op jit(solution)/shard_map/pallas_call | solution.py:676
  44.1 1.2 %shard_map.139 = (f32[2,8,1024]{2,1,0:T(8,128)}, f32[8,1024]{1,0:T(8,128)}, f32[8,128]{1,0:T(8,128)}, f32[4]{0:T(128)}) custom-call(f32[2,8,1024]{2,1,0:T(8,128)S(1)} %get-tuple-element.12.vel, f32[8,1024]{1,0:T(8,128)S(1)} %get-tuple-element.13.rho, f32[8,128]{1,0:T(8,128)S(1)} %get-tuple-element.14.eta, f32[1,128]{1,0:T(1,128)S(1)} %get-tuple-element.15.drift), custom_call_target="tpu_custom_call" | custom-call | tf_op jit(solution)/shard_map/pallas_call | solution.py:715

commit v7 on v6

--- a/solution.py
+++ b/solution.py
@@ -99,12 +99,15 @@
     coef,
     bsend,
     brecv,
+    hsend,
+    hrecv,
     lsem,
     usem,
     rsem,
     gsem,
     ssem,
     bsem,
+    hsem,
     zsem,
     tok,
 ):
@@ -124,18 +127,15 @@
     plane.sort(key=lambda ab: -2 * min(ab[0], X_CHIPS - ab[0]) - min(ab[1], n_level - ab[1]))
 
     barrier = pltpu.get_barrier_semaphore()
-    count = 0
 
     def greet(a, b):
         pl.semaphore_signal(barrier, inc=1, device_id=(a, b), device_id_type=MESH)
 
-    for d in far_first(n_level, 0):
-        greet(up, level_peers[d])
-        greet(down, level_peers[d])
-        count += 2
-        if d:
-            greet(p, level_peers[d])
-            count += 1
+    greet(up, g)
+    greet(down, g)
+    for d in far_first(n_level):
+        greet(p, level_peers[d])
+    count = n_level + 1
 
     inputs = [
         (send_hbm, send_ref),
@@ -223,7 +223,6 @@
         for side in range(2):
             got = listed_levels(tiles, side)
             rsend[s, side] = got
-            gsend[s, side, 0:1] = jnp.sum(got * th, axis=0, keepdims=True)
         for d in range(TILES):
             lsend[s, 0, d : d + 1] = jnp.sum(tiles[d] * th, axis=0, keepdims=True)
 
@@ -249,8 +248,6 @@
     list_velocity(0)
     list_density(0, 0)
     lsend[0, 1] = jnp.zeros((8, LANES), jnp.float32)
-    for side in range(2):
-        gsend[0, side, 1:2] = jnp.zeros((1, LANES), jnp.float32)
     loads[5].wait()
     wet_nodes = (bot_ref[...] > 0).astype(jnp.float32)
     eta[...] = eta_ref[...]
@@ -259,9 +256,8 @@
         ssend[side, 1:2] = listed_nodes(wet_nodes, side)
 
     pl.semaphore_wait(barrier, count)
+    send_density(0)
     send_velocity(0)
-    send_sums(0)
-    send_density(0)
     send_level(0)
     copy(ssend.at[0], srecv.at[1], ssem, 0, down, g).start()
     copy(ssend.at[1], srecv.at[0], ssem, 0, up, g).start()
@@ -325,6 +321,20 @@
             outs = [jnp.where(hit, lane_gather(a, idx), o) for a, o in zip(halo[side], outs)]
         return outs
 
+    def send_halo_mass():
+        for side in range(2):
+            hsend[side : side + 1] = jnp.sum(rrecv[0, side] * th, axis=0, keepdims=True)
+        for d in far_first(n_level):
+            copy(hsend, hrecv.at[d - 1], hsem, 0, p, level_peers[d]).start()
+
+    def halo_mass():
+        arrived(hrecv, hsem, 0)
+        zero = jnp.zeros((1, LANES), jnp.float32)
+        for side in range(2):
+            for d in range(n_level):
+                grecv[0, side, d, 0:1] = hrecv[d - 1, side : side + 1] if d else zero
+                grecv[0, side, d, 1:2] = zero
+
     def velocity_of(s, d):
         if d >= TILES:
             return usend[s, d - TILES, 0], usend[s, d - TILES, 1]
@@ -382,7 +392,6 @@
 
     def find_q(s):
         arrived(lrecv.at[s], lsem, s)
-        arrived(grecv.at[s], gsem, s)
         div, mass = lsend[s, 1], jnp.zeros((8, LANES), jnp.float32)
         for d in range(1, n_level):
             mass = mass + jnp.where(g >= d, lrecv[s, d - 1, 0], 0.0)
@@ -485,32 +494,47 @@
         par = lax.rem(s, 2)
         @pl.when(s == 1)
         def _():
-            pass_token(2)
+            pass_token(3)
+
+        gather_own(par, (*lists, *range(TILES)))
+
+        @pl.when(s == 0)
+        def _():
+            pass_token(1)
             drift_weights()
 
-        @pl.when(s == 2)
+        arrived(rrecv.at[s], rsem, s)
+
+        @pl.when(s == 0)
         def _():
-            pass_token(4)
-
-        gather_own(par, (*lists, *range(TILES)))
-        arrived(rrecv.at[s], rsem, s)
+            send_halo_mass()
+
         density_terms(s, par, lists)
         send_density(s + 1)
         density_terms(s, par, range(TILES))
 
         @pl.when(s == 0)
         def _():
-            pass_token(1)
+            pass_token(2)
             arrived(srecv, ssem, 0)
             etah[...] = srecv[:, 0]
 
         @pl.when(s == 1)
         def _():
-            pass_token(3)
+            pass_token(4)
 
         arrived(urecv.at[s], usem, s)
         velocity_terms(s, lists)
         send_sums(s + 1)
+
+        @pl.when(s == 0)
+        def _():
+            halo_mass()
+
+        @pl.when(s > 0)
+        def _():
+            arrived(grecv.at[s], gsem, s)
+
         find_q(s)
         shared_terms(lists)
         for side in range(2):
@@ -550,6 +574,7 @@
     arrived(urecv.at[last], usem, last)
     velocity_terms(last, range(TILES))
     send_level(STEPS)
+    arrived(grecv.at[last], gsem, last)
     find_q(last)
     shared_terms(range(TILES))
     for d in range(TILES):
@@ -569,24 +594,26 @@
         div = div + lrecv[STEPS, d - 1, 1]
     eta[...] = eta[...] - DT * wet_nodes * div
 
+    for s in range(STEPS + 1):
+        left(lrecv.at[s], lsem, s)
+    for s in range(STEPS):
+        left(usend.at[s], usem, s)
+        left(rsend.at[s], rsem, s)
+    for s in range(1, STEPS):
+        left(grecv.at[s], gsem, s)
+    left(ssend, ssem, 0)
+    left(bsend, bsem, 0)
+    left(hrecv, hsem, 0)
+    left(zrecv, zsem, 0)
+
     arrived(xrecv, zsem, 1)
     for i in range(len(plane)):
         row = row + xrecv[i]
     lane_row = lane[0:1]
     total = jnp.sum(jnp.where(lane_row == STEPS, row, 0.0), axis=1, keepdims=True)
-    drifts = jnp.where(lane_row < STEPS, row / total, 0.0)
-    drift_out[...] = drifts
-    eta_out[...] = eta[...] + DT * jnp.sum(drifts, axis=1, keepdims=True)
-
-    for s in range(STEPS + 1):
-        left(lrecv.at[s], lsem, s)
-    for s in range(STEPS):
-        left(usend.at[s], usem, s)
-        left(rsend.at[s], rsem, s)
-        left(grecv.at[s], gsem, s)
-    left(ssend, ssem, 0)
-    left(bsend, bsem, 0)
-    left(zrecv, zsem, 0)
+    drift_sum = jnp.sum(jnp.where(lane_row < STEPS, row, 0.0), axis=1, keepdims=True)
+    drift_out[...] = jnp.where(lane_row < STEPS, row / total, 0.0)
+    eta_out[...] = eta[...] + DT * (drift_sum / total)
     left(xrecv, zsem, 1)
 
 
@@ -668,6 +695,8 @@
             (2, 8, LANES),
             (2, 2, LANES),
             (2, 2, LANES),
+            (2, LANES),
+            (peers, 2, LANES),
         ]
 
         def body(*refs):
@@ -692,6 +721,7 @@
                 dma((2, 4)),
                 dma((2, 4)),
                 dma((2, 4)),
+                dma((2, 1)),
                 dma((2, 1)),
                 dma((2, 1)),
                 dma((2, 2)),

time: 45.5 us -> 46.5 us (1.022)
  Pallas kernels: 44.6 us -> 45.7 us
    pallas_call x1, Pallas kernels: 43.5 us -> 44.5 us  [local(): pl.pallas_call(body, out_shape=(pltpu.VMEM(velocity.shape, f32), pltpu.VM...]
where the time goes in v7:
time: 46.5 us; the launch traced here: 46.4 us
  Pallas kernels  45.7 us (98%)
  between operations  0.64 us (1%)
    pallas_call x1, Pallas kernels, local(): pl.pallas_call(body, out_shape=(pltpu.VMEM(velocity.shape, f32), pltpu.VM...  44.5 us
    pallas_call x1, Pallas kernels, local(): pl.pallas_call(finish, out_shape=(jax.ShapeDtypeStruct(velocity.shape, f3...  1.18 us

profile of v7, /device:TPU:1, one launch (start us, length us, event | category | flops | bytes accessed | tf_op | source)
XLA Modules:
  0.0 46.4 jit_solution(16019223319928210000)
XLA Ops:
  0.6 44.5 %shard_map.138 = (f32[2,8,1024]{2,1,0:T(8,128)S(1)}, f32[8,1024]{1,0:T(8,128)S(1)}, f32[8,128]{1,0:T(8,128)S(1)}, f32[1,128]{1,0:T(1,128)S(1)}) custom-call(f32[2,8,1024]{2,1,0:T(8,128)} %refs_0_.1, f32[8,1024]{1,0:T(8,128)} %refs_1_.1, f32[8,128]{1,0:T(8,128)} %bitcast.7, f32[6,2,1024]{2,1,0:T(2,128)} %bitcast.6, f32[6,1024]{1,0:T(8,128)} %refs_4_.1, ...), custom_call_target="tpu_custom_call" | custom-call | tf_op jit(solution)/shard_map/pallas_call | solution.py:705
  45.2 1.2 %shard_map.139 = (f32[2,8,1024]{2,1,0:T(8,128)}, f32[8,1024]{1,0:T(8,128)}, f32[8,128]{1,0:T(8,128)}, f32[4]{0:T(128)}) custom-call(f32[2,8,1024]{2,1,0:T(8,128)S(1)} %get-tuple-element.12.vel, f32[8,1024]{1,0:T(8,128)S(1)} %get-tuple-element.13.rho, f32[8,128]{1,0:T(8,128)S(1)} %get-tuple-element.14.eta, f32[1,128]{1,0:T(1,128)S(1)} %get-tuple-element.15.drift), custom_call_target="tpu_custom_call" | custom-call | tf_op jit(solution)/shard_map/pallas_call | solution.py:745

commit v8 on v6

--- a/solution.py
+++ b/solution.py
@@ -32,6 +32,12 @@
 
 def far_first(count, start=1):
     return sorted(range(start, count), key=lambda d: -min(d, count - d))
+
+
+def when(condition):
+    if isinstance(condition, bool):
+        return lambda act: act() if condition else None
+    return pl.when(condition)
 
 
 def wide(row):
@@ -259,9 +265,9 @@
         ssend[side, 1:2] = listed_nodes(wet_nodes, side)
 
     pl.semaphore_wait(barrier, count)
-    send_velocity(0)
     send_sums(0)
     send_density(0)
+    send_velocity(0)
     send_level(0)
     copy(ssend.at[0], srecv.at[1], ssem, 0, down, g).start()
     copy(ssend.at[1], srecv.at[0], ssem, 0, up, g).start()
@@ -481,67 +487,78 @@
                 total = total + wide(brecv[side, j : j + 1]) * usend[STEPS - 1, side, j]
         return total * th
 
+    def send_drift():
+        sums = jnp.zeros((8, LANES), jnp.float32)
+        terms = [vv[s] for s in range(STEPS - 1)]
+        terms += [early_drift(), area_ref[...] * wet_nodes * (1.0 / n_level)]
+        for j, term in enumerate(terms):
+            sums = jnp.where(sub == j, wide(jnp.sum(term, axis=0, keepdims=True)), sums)
+        sums = jnp.broadcast_to(jnp.sum(sums, axis=1, keepdims=True), (8, LANES))
+        zsend[...] = jnp.sum(jnp.where(sub == lane, sums, 0.0), axis=0, keepdims=True)
+        pl.semaphore_wait(tok.at[4], 2)
+        for d in far_first(n_z):
+            copy(zsend, zrecv.at[d - 1], zsem, 0, z_peer(d), g).start()
+
     def step(s, _):
         par = lax.rem(s, 2)
-        @pl.when(s == 1)
+        final = s == STEPS - 2 if isinstance(s, int) else False
+
+        @when(s == 1)
         def _():
-            pass_token(2)
+            pass_token(3)
+
+        gather_own(par, (*lists, *range(TILES)))
+
+        @when(s == 0)
+        def _():
+            pass_token(1)
             drift_weights()
 
-        @pl.when(s == 2)
-        def _():
-            pass_token(4)
-
-        gather_own(par, (*lists, *range(TILES)))
         arrived(rrecv.at[s], rsem, s)
         density_terms(s, par, lists)
         send_density(s + 1)
         density_terms(s, par, range(TILES))
 
-        @pl.when(s == 0)
+        @when(s == 0)
         def _():
-            pass_token(1)
+            pass_token(2)
             arrived(srecv, ssem, 0)
             etah[...] = srecv[:, 0]
 
-        @pl.when(s == 1)
+        @when(s == 1)
         def _():
-            pass_token(3)
+            pass_token(4)
 
         arrived(urecv.at[s], usem, s)
         velocity_terms(s, lists)
-        send_sums(s + 1)
+        if not final:
+            send_sums(s + 1)
         find_q(s)
         shared_terms(lists)
         for side in range(2):
             for c in range(2):
                 usend[s + 1, side, c] = new_velocity(TILES + side, c)
-        send_velocity(s + 1)
+        if not final:
+            send_velocity(s + 1)
         velocity_terms(s, range(TILES))
-        send_level(s + 1)
+        if not final:
+            send_level(s + 1)
         vv[s] = area_ref[...] * wet_nodes * lsend[s + 1, 1]
         shared_terms(range(TILES))
         for d in range(TILES):
             for c in range(2):
                 x[c, d] = new_velocity(d, c)
+        if final:
+            send_drift()
+            send_velocity(s + 1)
+            send_sums(s + 1)
+            send_level(s + 1)
         return 0
 
-    lax.fori_loop(0, STEPS - 1, step, 0)
+    lax.fori_loop(0, STEPS - 2, step, 0)
+    step(STEPS - 2, 0)
     last = STEPS - 1
     par = last % 2
-
-    sums = jnp.zeros((8, LANES), jnp.float32)
-    terms = [vv[s] for s in range(last)]
-    terms += [early_drift(), area_ref[...] * wet_nodes * (1.0 / n_level)]
-    for j, term in enumerate(terms):
-        sums = jnp.where(sub == j, wide(jnp.sum(term, axis=0, keepdims=True)), sums)
-    sums = jnp.broadcast_to(jnp.sum(sums, axis=1, keepdims=True), (8, LANES))
-    row = jnp.sum(jnp.where(sub == lane, sums, 0.0), axis=0, keepdims=True)
-    zsend[...] = row
-    pl.semaphore_wait(tok.at[4], 2)
-    for d in far_first(n_z):
-        copy(zsend, zrecv.at[d - 1], zsem, 0, z_peer(d), g).start()
-
     gather_own(par, range(TILES))
     arrived(rrecv.at[last], rsem, last)
     density_terms(last, par, range(TILES))
@@ -557,6 +574,7 @@
             vel_out[c, :, d * LANES : (d + 1) * LANES] = new_velocity(d, c)
 
     arrived(zrecv, zsem, 0)
+    row = zsend[...]
     for d in range(1, n_z):
         row = row + zrecv[d - 1]
     xsend[...] = row
@@ -568,15 +586,6 @@
     for d in range(1, n_level):
         div = div + lrecv[STEPS, d - 1, 1]
     eta[...] = eta[...] - DT * wet_nodes * div
-
-    arrived(xrecv, zsem, 1)
-    for i in range(len(plane)):
-        row = row + xrecv[i]
-    lane_row = lane[0:1]
-    total = jnp.sum(jnp.where(lane_row == STEPS, row, 0.0), axis=1, keepdims=True)
-    drifts = jnp.where(lane_row < STEPS, row / total, 0.0)
-    drift_out[...] = drifts
-    eta_out[...] = eta[...] + DT * jnp.sum(drifts, axis=1, keepdims=True)
 
     for s in range(STEPS + 1):
         left(lrecv.at[s], lsem, s)
@@ -587,6 +596,15 @@
     left(ssend, ssem, 0)
     left(bsend, bsem, 0)
     left(zrecv, zsem, 0)
+
+    arrived(xrecv, zsem, 1)
+    for i in range(len(plane)):
+        row = row + xrecv[i]
+    lane_row = lane[0:1]
+    total = jnp.sum(jnp.where(lane_row == STEPS, row, 0.0), axis=1, keepdims=True)
+    drift_sum = jnp.sum(jnp.where(lane_row < STEPS, row, 0.0), axis=1, keepdims=True)
+    drift_out[...] = jnp.where(lane_row < STEPS, row / total, 0.0)
+    eta_out[...] = eta[...] + DT * (drift_sum / total)
     left(xrecv, zsem, 1)
 
 

time: 45.5 us -> 45.1 us (level)
  no operation moved by 1% of the time
where the time goes in v8:
time: 45.1 us; the launch traced here: 44.9 us
  Pallas kernels  44.3 us (98%)
  between operations  0.64 us (1%)
    pallas_call x1, Pallas kernels, local(): pl.pallas_call(body, out_shape=(pltpu.VMEM(velocity.shape, f32), pltpu.VM...  43.1 us
    pallas_call x1, Pallas kernels, local(): pl.pallas_call(finish, out_shape=(jax.ShapeDtypeStruct(velocity.shape, f3...  1.18 us

profile of v8, /device:TPU:1, one launch (start us, length us, event | category | flops | bytes accessed | tf_op | source)
XLA Modules:
  0.0 44.9 jit_solution(18100409309056938112)
XLA Ops:
  0.6 43.1 %shard_map.138 = (f32[2,8,1024]{2,1,0:T(8,128)S(1)}, f32[8,1024]{1,0:T(8,128)S(1)}, f32[8,128]{1,0:T(8,128)S(1)}, f32[1,128]{1,0:T(1,128)S(1)}) custom-call(f32[2,8,1024]{2,1,0:T(8,128)} %refs_0_.1, f32[8,1024]{1,0:T(8,128)} %refs_1_.1, f32[8,128]{1,0:T(8,128)} %bitcast.7, f32[6,2,1024]{2,1,0:T(2,128)} %bitcast.6, f32[6,1024]{1,0:T(8,128)} %refs_4_.1, ...), custom_call_target="tpu_custom_call" | custom-call | tf_op jit(solution)/shard_map/pallas_call | solution.py:694
  43.7 1.2 %shard_map.139 = (f32[2,8,1024]{2,1,0:T(8,128)}, f32[8,1024]{1,0:T(8,128)}, f32[8,128]{1,0:T(8,128)}, f32[4]{0:T(128)}) custom-call(f32[2,8,1024]{2,1,0:T(8,128)S(1)} %get-tuple-element.12.vel, f32[8,1024]{1,0:T(8,128)S(1)} %get-tuple-element.13.rho, f32[8,128]{1,0:T(8,128)S(1)} %get-tuple-element.14.eta, f32[1,128]{1,0:T(1,128)S(1)} %get-tuple-element.15.drift), custom_call_target="tpu_custom_call" | custom-call | tf_op jit(solution)/shard_map/pallas_call | solution.py:733

commit v9 on v8

--- a/solution.py
+++ b/solution.py
@@ -500,13 +500,11 @@
             copy(zsend, zrecv.at[d - 1], zsem, 0, z_peer(d), g).start()
 
     def step(s, _):
-        par = lax.rem(s, 2)
+        par = s % 2 if isinstance(s, int) else lax.rem(s, 2)
         final = s == STEPS - 2 if isinstance(s, int) else False
 
-        @when(s == 1)
-        def _():
-            pass_token(3)
-
+        if final:
+            pass_token(4)
         gather_own(par, (*lists, *range(TILES)))
 
         @when(s == 0)
@@ -514,6 +512,10 @@
             pass_token(1)
             drift_weights()
 
+        @when(s == 1)
+        def _():
+            pass_token(3)
+
         arrived(rrecv.at[s], rsem, s)
         density_terms(s, par, lists)
         send_density(s + 1)
@@ -521,18 +523,15 @@
 
         @when(s == 0)
         def _():
-            pass_token(2)
             arrived(srecv, ssem, 0)
             etah[...] = srecv[:, 0]
-
-        @when(s == 1)
-        def _():
-            pass_token(4)
 
         arrived(urecv.at[s], usem, s)
         velocity_terms(s, lists)
         if not final:
             send_sums(s + 1)
+        if final:
+            velocity_terms(s, range(TILES))
         find_q(s)
         shared_terms(lists)
         for side in range(2):
@@ -540,14 +539,18 @@
                 usend[s + 1, side, c] = new_velocity(TILES + side, c)
         if not final:
             send_velocity(s + 1)
-        velocity_terms(s, range(TILES))
         if not final:
+            velocity_terms(s, range(TILES))
             send_level(s + 1)
         vv[s] = area_ref[...] * wet_nodes * lsend[s + 1, 1]
         shared_terms(range(TILES))
         for d in range(TILES):
             for c in range(2):
                 x[c, d] = new_velocity(d, c)
+        @when(s == 0)
+        def _():
+            pass_token(2)
+
         if final:
             send_drift()
             send_velocity(s + 1)

time: 45.1 us -> 44.9 us (level)
  no operation moved by 1% of the time
where the time goes in v9:
time: 44.9 us; the launch traced here: 44.7 us
  Pallas kernels  44.1 us (98%)
  between operations  0.64 us (1%)
    pallas_call x1, Pallas kernels, local(): pl.pallas_call(body, out_shape=(pltpu.VMEM(velocity.shape, f32), pltpu.VM...  42.9 us
    pallas_call x1, Pallas kernels, local(): pl.pallas_call(finish, out_shape=(jax.ShapeDtypeStruct(velocity.shape, f3...  1.18 us

profile of v9, /device:TPU:1, one launch (start us, length us, event | category | flops | bytes accessed | tf_op | source)
XLA Modules:
  0.0 44.7 jit_solution(5375231735413051025)
XLA Ops:
  0.6 42.9 %shard_map.138 = (f32[2,8,1024]{2,1,0:T(8,128)S(1)}, f32[8,1024]{1,0:T(8,128)S(1)}, f32[8,128]{1,0:T(8,128)S(1)}, f32[1,128]{1,0:T(1,128)S(1)}) custom-call(f32[2,8,1024]{2,1,0:T(8,128)} %refs_0_.1, f32[8,1024]{1,0:T(8,128)} %refs_1_.1, f32[8,128]{1,0:T(8,128)} %bitcast.7, f32[6,2,1024]{2,1,0:T(2,128)} %bitcast.6, f32[6,1024]{1,0:T(8,128)} %refs_4_.1, ...), custom_call_target="tpu_custom_call" | custom-call | tf_op jit(solution)/shard_map/pallas_call | solution.py:697
  43.6 1.2 %shard_map.139 = (f32[2,8,1024]{2,1,0:T(8,128)}, f32[8,1024]{1,0:T(8,128)}, f32[8,128]{1,0:T(8,128)}, f32[4]{0:T(128)}) custom-call(f32[2,8,1024]{2,1,0:T(8,128)S(1)} %get-tuple-element.12.vel, f32[8,1024]{1,0:T(8,128)S(1)} %get-tuple-element.13.rho, f32[8,128]{1,0:T(8,128)S(1)} %get-tuple-element.14.eta, f32[1,128]{1,0:T(1,128)S(1)} %get-tuple-element.15.drift), custom_call_target="tpu_custom_call" | custom-call | tf_op jit(solution)/shard_map/pallas_call | solution.py:736

commit v10 on v9

--- a/solution.py
+++ b/solution.py
@@ -38,6 +38,12 @@
     if isinstance(condition, bool):
         return lambda act: act() if condition else None
     return pl.when(condition)
+
+
+def tree_sum(terms):
+    while len(terms) > 1:
+        terms = [sum(terms[i + 1 : i + 2], terms[i]) for i in range(0, len(terms), 2)]
+    return terms[0]
 
 
 def wide(row):
@@ -479,20 +485,25 @@
 
     def early_drift():
         arrived(brecv, bsem, 0)
-        total = jnp.zeros((8, LANES), jnp.float32)
+        terms = []
         for j in range(2):
             for d in range(TILES):
-                total = total + wide(coef[j, d : d + 1]) * x[j, d]
+                terms.append(wide(coef[j, d : d + 1]) * x[j, d])
             for side in range(2):
-                total = total + wide(brecv[side, j : j + 1]) * usend[STEPS - 1, side, j]
-        return total * th
-
-    def send_drift():
+                terms.append(wide(brecv[side, j : j + 1]) * usend[STEPS - 1, side, j])
+        return tree_sum(terms) * th
+
+    def earlier_drifts():
         sums = jnp.zeros((8, LANES), jnp.float32)
-        terms = [vv[s] for s in range(STEPS - 1)]
-        terms += [early_drift(), area_ref[...] * wet_nodes * (1.0 / n_level)]
-        for j, term in enumerate(terms):
+        terms = [(s, vv[s]) for s in range(STEPS - 1)]
+        terms += [(STEPS, area_ref[...] * wet_nodes * (1.0 / n_level))]
+        for j, term in terms:
             sums = jnp.where(sub == j, wide(jnp.sum(term, axis=0, keepdims=True)), sums)
+        return sums
+
+    def send_drift(sums):
+        row = jnp.sum(early_drift(), axis=0, keepdims=True)
+        sums = jnp.where(sub == STEPS - 1, wide(row), sums)
         sums = jnp.broadcast_to(jnp.sum(sums, axis=1, keepdims=True), (8, LANES))
         zsend[...] = jnp.sum(jnp.where(sub == lane, sums, 0.0), axis=0, keepdims=True)
         pl.semaphore_wait(tok.at[4], 2)
@@ -532,6 +543,8 @@
             send_sums(s + 1)
         if final:
             velocity_terms(s, range(TILES))
+            vv[s] = area_ref[...] * wet_nodes * lsend[s + 1, 1]
+            sums = earlier_drifts()
         find_q(s)
         shared_terms(lists)
         for side in range(2):
@@ -542,7 +555,7 @@
         if not final:
             velocity_terms(s, range(TILES))
             send_level(s + 1)
-        vv[s] = area_ref[...] * wet_nodes * lsend[s + 1, 1]
+            vv[s] = area_ref[...] * wet_nodes * lsend[s + 1, 1]
         shared_terms(range(TILES))
         for d in range(TILES):
             for c in range(2):
@@ -552,7 +565,7 @@
             pass_token(2)
 
         if final:
-            send_drift()
+            send_drift(sums)
             send_velocity(s + 1)
             send_sums(s + 1)
             send_level(s + 1)
@@ -577,9 +590,7 @@
             vel_out[c, :, d * LANES : (d + 1) * LANES] = new_velocity(d, c)
 
     arrived(zrecv, zsem, 0)
-    row = zsend[...]
-    for d in range(1, n_z):
-        row = row + zrecv[d - 1]
+    row = tree_sum([zsend[...]] + [zrecv[d] for d in range(n_z - 1)])
     xsend[...] = row
     for i, (a, b) in enumerate(plane):
         copy(xsend, xrecv.at[i], zsem, 1, x_peers[a], level_peers[b]).start()
@@ -601,8 +612,7 @@
     left(zrecv, zsem, 0)
 
     arrived(xrecv, zsem, 1)
-    for i in range(len(plane)):
-        row = row + xrecv[i]
+    row = tree_sum([row] + [xrecv[i] for i in range(len(plane))])
     lane_row = lane[0:1]
     total = jnp.sum(jnp.where(lane_row == STEPS, row, 0.0), axis=1, keepdims=True)
     drift_sum = jnp.sum(jnp.where(lane_row < STEPS, row, 0.0), axis=1, keepdims=True)

time: 44.9 us -> 44.9 us (level)
  no operation moved by 1% of the time
where the time goes in v10:
time: 44.9 us; the launch traced here: 44.7 us
  Pallas kernels  44.1 us (98%)
  between operations  0.64 us (1%)
    pallas_call x1, Pallas kernels, local(): pl.pallas_call(body, out_shape=(pltpu.VMEM(velocity.shape, f32), pltpu.VM...  42.9 us
    pallas_call x1, Pallas kernels, local(): pl.pallas_call(finish, out_shape=(jax.ShapeDtypeStruct(velocity.shape, f3...  1.18 us

profile of v10, /device:TPU:1, one launch (start us, length us, event | category | flops | bytes accessed | tf_op | source)
XLA Modules:
  0.0 44.7 jit_solution(5379180422758370317)
XLA Ops:
  0.6 42.9 %shard_map.138 = (f32[2,8,1024]{2,1,0:T(8,128)S(1)}, f32[8,1024]{1,0:T(8,128)S(1)}, f32[8,128]{1,0:T(8,128)S(1)}, f32[1,128]{1,0:T(1,128)S(1)}) custom-call(f32[2,8,1024]{2,1,0:T(8,128)} %refs_0_.1, f32[8,1024]{1,0:T(8,128)} %refs_1_.1, f32[8,128]{1,0:T(8,128)} %bitcast.7, f32[6,2,1024]{2,1,0:T(2,128)} %bitcast.6, f32[6,1024]{1,0:T(8,128)} %refs_4_.1, ...), custom_call_target="tpu_custom_call" | custom-call | tf_op jit(solution)/shard_map/pallas_call | solution.py:707
  43.5 1.2 %shard_map.139 = (f32[2,8,1024]{2,1,0:T(8,128)}, f32[8,1024]{1,0:T(8,128)}, f32[8,128]{1,0:T(8,128)}, f32[4]{0:T(128)}) custom-call(f32[2,8,1024]{2,1,0:T(8,128)S(1)} %get-tuple-element.12.vel, f32[8,1024]{1,0:T(8,128)S(1)} %get-tuple-element.13.rho, f32[8,128]{1,0:T(8,128)S(1)} %get-tuple-element.14.eta, f32[1,128]{1,0:T(1,128)S(1)} %get-tuple-element.15.drift), custom_call_target="tpu_custom_call" | custom-call | tf_op jit(solution)/shard_map/pallas_call | solution.py:746
